TPU v7x, 256 devices: a whole 4x4x8 slice. The times are simulated.
256 devices in a mesh: dp: 32 (over y, z), mp: 8 (over x, core).
Axes of the slice: x: 4, y: 4, z: 8, core: 2. Of those that a mesh axis runs over, the one named last changes fastest.
Arguments:
- queries: bfloat16 [1024, 64, 16, 128], P('dp', 'mp'), may hold values from -5 to 5
- draft_kv: bfloat16 [1024, 2, 8, 16, 128], P('dp', None, 'mp'), may hold values from -5 to 5
- kv_pool: bfloat16 [16384, 2, 8, 16, 128], P('dp', None, 'mp'), may hold values from -5 to 5
- block_dest: int32 [16384], P('dp'), may hold values from -1 to 31, as said below
- block_table: int32 [1024, 32], P('dp'), may hold values from 0 to 1023, as said below
- context_len: int32 [1024], P('dp'), may hold values from 0 to 512
- draft_len: int32 [1024], P('dp'), may hold values from 2 to 16
- accept_mask: int32 [1024, 16], P('dp'), may hold values 0 or 1
- out_weight: bfloat16 [8192, 4096], P('mp'), may hold values from -0.5 to 0.5
- residual: bfloat16 [16384, 4096], P('dp'), may hold values from -80 to 80
- norm_gain: float32 [4096], P('mp'), may hold values from 0.1 to 1.9
Outputs:
- normed: bfloat16 [16384, 4096], P('dp', 'mp')
Inputs may be any that keep to these rules, and one draw needn't show every extreme that they name: Pool block b belongs to rank b // 512 and goes to rank block_dest[b]; -1 marks a free block. A rank sends at most 32 blocks to one rank, and some rank receives exactly 32 blocks from every rank. `block_table`: entry e of request r is read where e * 16 < context_len[r]. Such an entry names slot s * 32 + k of the blocks received by rank r // 32, one that holds a block (the k-th, in pool order, that rank s sends there); the entries read on one rank name distinct slots, and every received block is named by one of them.
All inputs are finite; a program needn't handle non-finite values. No bound on the sum of `accept_mask` on one device may be relied on, other than what follows from the above.
Results may differ from a plain program's by a relative error of at most 0.011.
Values may be sent and summed in bfloat16 or wider, within the bound.
No kernel may reach another device: no remote copies, remote signals or barrier semaphores. Data moves between devices by JAX's collectives and lax.ppermute only.
A program may use at most 192 MiB of HBM per device.

v0:
```python
import math

import jax
import jax.numpy as jnp
from jax import lax
from jax.sharding import PartitionSpec as P

masked_score = -1e30
norm_epsilon = 1e-05


def from_everyone(array, axis):
    length = lax.axis_size(axis)
    return lax.all_to_all(
        jnp.broadcast_to(array[None], (length, *array.shape)), axis, 0, 0, tiled=True
    )


def over_copies(array, axis):
    everything = from_everyone(array, axis)
    return jnp.sum(everything, axis=0)


def on_device(
    queries,
    draft_kv,
    kv_pool,
    block_dest,
    block_table,
    context_len,
    draft_len,
    accept_mask,
    out_weight,
    residual,
    norm_gain,
):
    rank_count = lax.axis_size("dp")
    pool_count = kv_pool.shape[0]
    capacity = 2 * pool_count // rank_count
    requests, heads_local, window, head_dim = queries.shape
    kv_local = draft_kv.shape[2]
    group_size = heads_local // kv_local
    block_len = kv_pool.shape[3]
    table_width = block_table.shape[1]
    scale_factor = 1.0 / math.sqrt(head_dim)
    destinations = jnp.arange(rank_count, dtype=jnp.int32)
    onehot = (block_dest[:, None] == destinations[None, :]).astype(jnp.int32)
    earlier = jnp.cumsum(onehot, axis=0, dtype=jnp.int32) - onehot
    order_in = jnp.sum(earlier * onehot, axis=1, dtype=jnp.int32)
    target = jnp.where(block_dest >= 0, block_dest * capacity + order_in, rank_count * capacity)
    outgoing = (
        jnp.zeros((rank_count * capacity,) + kv_pool.shape[1:], jnp.bfloat16)
        .at[target]
        .set(kv_pool, mode="drop")
    )
    arrived = lax.all_to_all(outgoing, "dp", split_axis=0, concat_axis=0, tiled=True)
    kept_count = jnp.sum(jnp.cumprod(accept_mask, axis=1, dtype=jnp.int32), axis=1, dtype=jnp.int32)
    visible = context_len - window + kept_count
    gathered = arrived[block_table]
    cached_keys = gathered[:, :, 0]
    cached_values = gathered[:, :, 1]
    grouped = queries.reshape(requests, kv_local, group_size, window, head_dim)
    cached = (
        jnp.einsum("rkgwd,rbkpd->rkgwbp", grouped, cached_keys, preferred_element_type=jnp.float32)
        * scale_factor
    )
    cached = cached.reshape(requests, kv_local, group_size, window, table_width * block_len)
    positions = jnp.arange(table_width * block_len, dtype=jnp.int32)
    readable = positions[None, :] < visible[:, None]
    cached = jnp.where(readable[:, None, None, None, :], cached, masked_score)
    draft_scores = (
        jnp.einsum("rkgwd,rkjd->rkgwj", grouped, draft_kv[:, 0], preferred_element_type=jnp.float32)
        * scale_factor
    )
    causal = (
        jnp.arange(window, dtype=jnp.int32)[None, :] <= jnp.arange(window, dtype=jnp.int32)[:, None]
    )
    draft_scores = jnp.where(causal[None, None, None], draft_scores, masked_score)
    row_max = jnp.maximum(jnp.max(cached, axis=4), jnp.max(draft_scores, axis=4))
    cached_exp = jnp.exp(cached - row_max[..., None])
    draft_exp = jnp.exp(draft_scores - row_max[..., None])
    denominator = jnp.sum(cached_exp, axis=4) + jnp.sum(draft_exp, axis=4)
    cached_prob = (cached_exp / denominator[..., None]).astype(jnp.bfloat16)
    cached_prob = cached_prob.reshape(
        requests, kv_local, group_size, window, table_width, block_len
    )
    draft_prob = (draft_exp / denominator[..., None]).astype(jnp.bfloat16)
    attended = jnp.einsum(
        "rkgwbp,rbkpd->rkgwd", cached_prob, cached_values, preferred_element_type=jnp.float32
    )
    attended = attended + jnp.einsum(
        "rkgwj,rkjd->rkgwd", draft_prob, draft_kv[:, 1], preferred_element_type=jnp.float32
    )
    token_rows = (
        attended.astype(jnp.bfloat16)
        .transpose(0, 3, 1, 2, 4)
        .reshape(requests * window, heads_local * head_dim)
    )
    partial_value = jnp.dot(token_rows, out_weight, preferred_element_type=jnp.float32)
    column_count = norm_gain.shape[0]
    column_start = lax.axis_index("mp") * column_count
    live_rows = (jnp.arange(window, dtype=jnp.int32)[None, :] < draft_len[:, None]).reshape(
        requests * window
    )
    share = lax.psum_scatter(
        partial_value.astype(jnp.bfloat16), "mp", scatter_dimension=1, tiled=True
    ).astype(jnp.float32)
    local_residual = lax.dynamic_slice_in_dim(residual, column_start, column_count, 1)
    local_hidden = local_residual.astype(jnp.float32) + share
    squares = over_copies(jnp.sum(local_hidden * local_hidden, axis=1), "mp")
    mean_square = (squares / (column_count * lax.axis_size("mp")))[:, None]
    normed = local_hidden * lax.rsqrt(mean_square + norm_epsilon) * norm_gain[None, :]
    return jnp.where(live_rows[:, None], normed, 0.0).astype(jnp.bfloat16)


def solution(mesh):
    return jax.shard_map(
        on_device,
        mesh=mesh,
        in_specs=(
            P("dp", "mp", None, None),
            P("dp", None, "mp", None, None),
            P("dp", None, "mp", None, None),
            P("dp"),
            P("dp", None),
            P("dp"),
            P("dp"),
            P("dp", None),
            P("mp", None),
            P("dp", None),
            P("mp"),
        ),
        out_specs=P("dp", "mp"),
        check_vma=False,
    )
```

profile of v0, /device:TPU:1, one launch (start us, length us, event | category | flops | bytes accessed | tf_op | source)
XLA Modules:
  0.0 446.1 jit_solution(13835461914624403804)
XLA Ops:
  6.5 0.8 fusion.24
  7.3 1.2 reduce-window.6
  8.7 0.8 fusion.23
  9.5 0.7 compare_select_fusion.1
  10.2 4.3 broadcast.107
  14.5 58.8 %scatter_fusion = bf16[1024,2,16,128]{3,2,1,0:T(8,128)(2,1)} fusion(bf16[1024,2,16,128]{3,2,1,0:T(8,128)(2,1)} %broadcast.107, s32[512]{0:T(512)S(1)} %compare_select_fusion.1, bf16[512,2,16,128]{3,2,1,0:T(8,128)(2,1)} %bitcast.103), kind=kCustom, calls=%fused_computation.1 | custom fusion | bytes 12584960 | tf_op jit(solution)/shard_map/scatter | solution.py:54
  73.3 12.3 %all-to-all-start = ((bf16[1024,2,1,16,128]{4,3,1,2,0:T(8,128)(2,1)}), bf16[1024,2,1,16,128]{4,3,1,2,0:T(8,128)(2,1)}, u32[]{:S(2)}, u32[]{:S(2)}) async-start(bf16[1024,2,1,16,128]{4,3,1,2,0:T(8,128)(2,1)} %bitcast.100), calls=%async_computation | async-start | bytes 16777216 | tf_op jit(solution)/shard_map/all_to_all | solution.py:56
  86.3 3.5 fusion.5
  89.8 184.0 %all-to-all-done = bf16[1024,2,1,16,128]{4,3,1,2,0:T(8,128)(2,1)} async-done(((bf16[1024,2,1,16,128]{4,3,1,2,0:T(8,128)(2,1)}), bf16[1024,2,1,16,128]{4,3,1,2,0:T(8,128)(2,1)}, u32[]{:S(2)}, u32[]{:S(2)}) %all-to-all-start) | async-done | bytes 8388640 | tf_op jit(solution)/shard_map/all_to_all | solution.py:56
  273.8 13.3 %gather_fusion = bf16[1024,2,16,128]{3,2,1,0:T(8,128)(2,1)} fusion(bf16[1024,2,16,128]{3,2,1,0:T(8,128)(2,1)} %bitcast.4, s32[1024]{0:T(1024)S(1)} %broadcast_clamp_fusion), kind=kCustom, calls=%fused_computation | custom fusion | bytes 16781312 | tf_op jit(solution)/shard_map/gather | solution.py:59
  287.1 8.0 %copy.45 = bf16[1024,2,16,128]{3,2,0,1:T(8,128)(2,1)} copy(bf16[1024,2,16,128]{3,2,1,0:T(8,128)(2,1)} %gather_fusion) | data formatting | bytes 16777216 | tf_op jit(solution)/shard_map/gather | solution.py:59
  295.1 25.9 %bitcast_reduce_fusion = (f32[32,8,16]{2,1,0:T(8,128)S(1)}, f32[32,32,16,8,16]{4,2,3,1,0:T(8,128)}) fusion(pred[32,32,16]{2,1,0:T(8,128)(4,1)S(1)} %broadcast_compare_fusion, bf16[32,8,16,128]{3,2,1,0:T(8,128)(2,1)S(1)} %copy-done, bf16[32,32,2,1,16,128]{5,4,1,0,3,2:T(8,128)(2,1)} %bitcast.101), kind=kOutput, calls=%fused_computation.3 | convolution fusion | flops 543158272 | bytes 13664256 | tf_op jit(solution)/shard_map/rkgwd,rbkpd->rkgwbp/dot_general | solution.py:64
  321.0 21.5 %fusion.1 = f32[32,8,16]{2,1,0:T(8,128)S(1)} fusion(f32[32,32,16,8,16]{4,2,3,1,0:T(8,128)} %get-tuple-element.6, f32[32,8,16]{2,1,0:T(8,128)S(1)} %max.9, pred[32,32,16]{2,1,0:T(8,128)(4,1)S(1)} %broadcast_compare_fusion), kind=kLoop, calls=%fused_computation.7 | loop fusion | flops 8384512 | bytes 8437760 | tf_op jit(solution)/shard_map/reduce_sum | solution.py:82
  342.5 0.9 fusion.6
  343.4 0.7 add.56
  344.0 28.7 %fusion.2 = f32[32,8,16,128,1]{3,2,1,4,0:T(8,128)} fusion(f32[32,32,16,8,16]{4,2,3,1,0:T(8,128)} %get-tuple-element.6, f32[32,8,16]{2,1,0:T(8,128)} %add.56, f32[32,8,16]{2,1,0:T(8,128)S(1)} %max.9, pred[32,32,16]{2,1,0:T(8,128)(4,1)S(1)} %broadcast_compare_fusion, bf16[32,32,2,1,16,128]{5,4,1,0,3,2:T(8,128)(2,1)} %bitcast.102), kind=kOutput, calls=%fused_computation.8 | convolution fusion | flops 547356672 | bytes 73564160 | tf_op jit(solution)/shard_map/rkgwbp,rbkpd->rkgwd/dot_general | solution.py:88
  372.8 2.6 fusion.7
  375.7 1.2 copy-done.6
  376.9 6.1 %convolution_convert_fusion = bf16[512,4096]{1,0:T(8,128)(2,1)} fusion(bf16[1024,4096]{1,0:T(8,128)(2,1)S(1)} %copy-done.6, bf16[64,8,8,128]{3,2,1,0:T(8,128)(2,1)S(1)} %bitcast.104), kind=kOutput, calls=%fused_computation.9 | convolution fusion | flops 4297064448 | bytes 13631488 | tf_op jit(solution)/shard_map/dot_general | solution.py:99
  383.0 40.6 %reduce-scatter.2.cloned.1.call-done = bf16[512,512]{1,0:T(8,128)(2,1)} async-done(((bf16[512,4096]{1,0:T(8,128)(2,1)}), bf16[512,512]{1,0:T(8,128)(2,1)}) %reduce-scatter.2.cloned.1.call-update) | async-done | bytes 524304 | tf_op jit(solution)/shard_map/reduce_scatter | solution.py:105
  423.5 1.4 multiply_reduce_fusion
  425.6 6.6 %all-to-all-start.1 = ((f32[8,1,512]{2,1,0:T(1,128)}), f32[8,1,512]{2,1,0:T(1,128)S(1)}, u32[]{:S(2)}, u32[]{:S(2)}) async-start(f32[8,1,512]{2,1,0:T(1,128)} %broadcast_in_dim.80), calls=%async_computation.2 | async-start | bytes 32768 | tf_op jit(solution)/shard_map/all_to_all | solution.py:14
  432.4 4.5 %all-to-all-done.1 = f32[8,1,512]{2,1,0:T(1,128)S(1)} async-done(((f32[8,1,512]{2,1,0:T(1,128)}), f32[8,1,512]{2,1,0:T(1,128)S(1)}, u32[]{:S(2)}, u32[]{:S(2)}) %all-to-all-start.1) | async-done | bytes 16416 | tf_op jit(solution)/shard_map/all_to_all | solution.py:14
  437.0 2.3 select_convert_fusion
  (37 shorter events, 2.1 us)
Async XLA Ops:
  6.5 79.8 %copy-start = (bf16[32,8,16,128]{3,2,1,0:T(8,128)(2,1)S(1)}, bf16[32,8,16,128]{3,2,1,0:T(8,128)(2,1)}, u32[]{:S(2)}) copy-start(bf16[32,8,16,128]{3,2,1,0:T(8,128)(2,1)} %param.11) | copy-start | bytes 3145732
  73.3 12.3 %copy-start.2 = (s32[32,32]{1,0:T(8,128)S(1)}, s32[32,32]{1,0:T(8,128)}, u32[]{:S(2)}) copy-start(s32[32,32]{1,0:T(8,128)} %param.15) | copy-start | bytes 12292
  73.3 12.4 %copy-start.3 = (s32[32,16]{0,1:T(8,128)S(1)}, s32[32,16]{0,1:T(8,128)}, u32[]{:S(2)}) copy-start(s32[32,16]{0,1:T(8,128)} %param.18) | copy-start | bytes 6148
  73.3 12.8 %copy-start.7 = (s32[32]{0:T(128)S(1)}, s32[32]{0:T(128)}, u32[]{:S(2)}) copy-start(s32[32]{0:T(128)} %param.16) | copy-start | bytes 388
  73.3 200.5 %all-to-all-start = ((bf16[1024,2,1,16,128]{4,3,1,2,0:T(8,128)(2,1)}), bf16[1024,2,1,16,128]{4,3,1,2,0:T(8,128)(2,1)}, u32[]{:S(2)}, u32[]{:S(2)}) async-start(bf16[1024,2,1,16,128]{4,3,1,2,0:T(8,128)(2,1)} %bitcast.100), calls=%async_computation | async-start | bytes 16777216 | tf_op jit(solution)/shard_map/all_to_all | solution.py:56
  85.6 338.0 %reduce-scatter.2.cloned.1.call-start = ((), (), s32[]{:S(2)}) async-start(), calls=%async_computation.3 | async-start | bytes 4718592 | tf_op jit(solution)/shard_map/reduce_scatter | solution.py:105
  344.0 28.7 %copy-start.1 = (f32[32,8,16]{2,1,0:T(8,128)S(1)}, f32[32,8,16]{2,1,0:T(8,128)}, u32[]{:S(2)}) copy-start(f32[32,8,16]{2,1,0:T(8,128)} %add.56) | copy-start | bytes 49156
  372.8 4.1 copy-start.6
  376.9 55.4 %copy-start.5 = (s32[32]{0:T(128)S(1)}, s32[32]{0:T(128)}, u32[]{:S(2)}) copy-start(s32[32]{0:T(128)} %param.17) | copy-start | bytes 388
  376.9 60.1 %copy-start.4 = (f32[512]{0:T(512)S(1)}, f32[512]{0:T(512)}, u32[]{:S(2)}) copy-start(f32[512]{0:T(512)} %param.21) | copy-start | bytes 6148
  425.6 11.3 %all-to-all-start.1 = ((f32[8,1,512]{2,1,0:T(1,128)}), f32[8,1,512]{2,1,0:T(1,128)S(1)}, u32[]{:S(2)}, u32[]{:S(2)}) async-start(f32[8,1,512]{2,1,0:T(1,128)} %broadcast_in_dim.80), calls=%async_computation.2 | async-start | bytes 32768 | tf_op jit(solution)/shard_map/all_to_all | solution.py:14
Sparse Core Ops, SparseCore 0:
  383.1 40.4 reduce-scatter.1
where the time goes:
time: 447 us; the launch traced here: 446 us
  waiting for transfers between devices  229 us (51%)
  local copies, waits for them, and re-layouts  86.9 us (19%)
  matrix products  66.8 us (15%)
  other arithmetic  30.8 us (7%)
  starting transfers between devices  19 us (4%)
  between operations  13.5 us (3%)
    all_to_all x1, waiting for transfers between devices, on_device(): lax.all_to_all(outgoing, 'dp', split_axis=0, concat_axis=0, tiled=True)  184 us
    scatter x1, local copies, waits for them, and re-layouts, on_device(): outgoing = jnp.zeros((rank_count * capacity,) + kv_pool.shape[1:], jnp.bf...  58.8 us
    reduce_scatter x1, waiting for transfers between devices, on_device(): lax.psum_scatter(partial_value.astype(jnp.bfloat16), 'mp', scatter_dimens...  40.6 us
    dot_general x1, matrix products, on_device(): jnp.einsum('rkgwbp,rbkpd->rkgwd', cached_prob, cached_values, preferred_e...  28.7 us
    dot_general x1, matrix products, on_device(): jnp.einsum('rkgwd,rbkpd->rkgwbp', grouped, cached_keys, preferred_element...  25.9 us
    reduce_sum x2, other arithmetic, on_device(): denominator = jnp.sum(cached_exp, axis=4) + jnp.sum(draft_exp, axis=4)  22.4 us
    gather x2, local copies, waits for them, and re-layouts, on_device(): gathered = arrived[block_table]  21.3 us
    all_to_all x1, starting transfers between devices, on_device(): lax.all_to_all(outgoing, 'dp', split_axis=0, concat_axis=0, tiled=True)  12.3 us
  transfers between devices with their start and end apart: 3, of which 3 were waited for; matrix products, arithmetic and copies ran while one was open for 1% of the time, Pallas kernels for 0%

commit v1 on v0

v1 whole, which is shorter than its diff:
```python
import functools
import math

import jax
import jax.numpy as jnp
from jax import lax
from jax.experimental import pallas as pl
from jax.experimental.pallas import tpu as pltpu
from jax.sharding import PartitionSpec as P

masked_score = -1e30
norm_epsilon = 1e-05
load_pieces = 8


def from_everyone(array, axis):
    length = lax.axis_size(axis)
    return lax.all_to_all(
        jnp.broadcast_to(array[None], (length, *array.shape)), axis, 0, 0, tiled=True
    )


def over_copies(array, axis):
    everything = from_everyone(array, axis)
    return jnp.sum(everything, axis=0)


def pack_kernel(rank_count, capacity, dest_ref, pool_ref, out_ref, staged, used, load_sem, store_sem):
    blocks = pool_ref.shape[0]
    piece = blocks // load_pieces

    def load(p):
        rows = pl.ds(p * piece, piece)
        return pltpu.make_async_copy(pool_ref.at[rows], staged.at[rows], load_sem.at[p])

    for p in range(load_pieces):
        load(p).start()

    def clear(d, carry):
        used[d] = 0
        return carry

    lax.fori_loop(0, rank_count, clear, 0)

    def store(b, slot):
        return pltpu.make_async_copy(staged.at[b], out_ref.at[slot], store_sem)

    def place(b, sent):
        d = dest_ref[b]
        live = d >= 0

        @pl.when(live)
        def _():
            k = used[d]
            used[d] = k + 1
            store(b, d * capacity + k).start()

        return sent + live.astype(jnp.int32)

    sent = jnp.int32(0)
    for p in range(load_pieces):
        load(p).wait()
        sent = lax.fori_loop(p * piece, (p + 1) * piece, place, sent, unroll=4)

    def drain(i, carry):
        store(0, 0).wait()
        return carry

    lax.fori_loop(0, sent, drain, 0)


def pack_blocks(block_dest, pool, rank_count, capacity):
    return pl.pallas_call(
        functools.partial(pack_kernel, rank_count, capacity),
        out_shape=jax.ShapeDtypeStruct((rank_count * capacity,) + pool.shape[1:], pool.dtype),
        in_specs=[
            pl.BlockSpec(memory_space=pltpu.SMEM),
            pl.BlockSpec(memory_space=pl.ANY),
        ],
        out_specs=pl.BlockSpec(memory_space=pl.ANY),
        scratch_shapes=[
            pltpu.VMEM(pool.shape, pool.dtype),
            pltpu.SMEM((rank_count,), jnp.int32),
            pltpu.SemaphoreType.DMA((load_pieces,)),
            pltpu.SemaphoreType.DMA,
        ],
        cost_estimate=pl.CostEstimate(flops=0, bytes_accessed=1 << 23, transcendentals=0),
        name="pack_blocks",
    )(block_dest, pool)


def attend_kernel(per_step, table_ref, visible_ref, queries_ref, draft_ref, arrived_ref, out_ref, cache, load_sem):
    slots = arrived_ref.shape[0]
    step = pl.program_id(0)
    width = table_ref.shape[0] // visible_ref.shape[0]
    block_len = arrived_ref.shape[1] // 2
    rows, head_dim = queries_ref.shape[1:]
    window = out_ref.shape[0] // per_step
    log_scale = math.log2(math.e) / math.sqrt(head_dim)

    @pl.when(step == 0)
    def _():
        piece = slots // load_pieces
        copies = [
            pltpu.make_async_copy(
                arrived_ref.at[pl.ds(p * piece, piece)],
                cache.at[pl.ds(p * piece, piece)],
                load_sem.at[p],
            )
            for p in range(load_pieces)
        ]
        for copy in copies:
            copy.start()
        cache[slots] = jnp.zeros_like(cache[slots])
        for copy in copies:
            copy.wait()

    positions = lax.broadcasted_iota(jnp.int32, (rows, width * block_len), 1)
    query_place = lax.broadcasted_iota(jnp.int32, (rows, window), 0) % window
    causal = lax.broadcasted_iota(jnp.int32, (rows, window), 1) <= query_place
    over_last = (((1,), (1,)), ((), ()))
    for n in range(per_step):
        request = step * per_step + n
        visible = visible_ref[request]
        places = [
            jnp.where(e * block_len < visible, table_ref[request * width + e], slots)
            for e in range(width)
        ]
        keys = jnp.concatenate([cache[s, :block_len, :] for s in places], axis=0)
        values = jnp.concatenate([cache[s, block_len:, :] for s in places], axis=0)
        query = queries_ref[n]
        cached = lax.dot_general(query, keys, over_last, preferred_element_type=jnp.float32)
        cached = jnp.where(positions < visible, cached, masked_score)
        drafts = lax.dot_general(
            query, draft_ref[n, :window, :], over_last, preferred_element_type=jnp.float32
        )
        drafts = jnp.where(causal, drafts, masked_score)
        row_max = jnp.maximum(
            jnp.max(cached, axis=1, keepdims=True), jnp.max(drafts, axis=1, keepdims=True)
        )
        cached = jnp.exp2((cached - row_max) * log_scale)
        drafts = jnp.exp2((drafts - row_max) * log_scale)
        denominator = jnp.sum(cached, axis=1, keepdims=True) + jnp.sum(drafts, axis=1, keepdims=True)
        attended = jnp.dot(cached.astype(jnp.bfloat16), values, preferred_element_type=jnp.float32)
        attended = attended + jnp.dot(
            drafts.astype(jnp.bfloat16), draft_ref[n, window:, :], preferred_element_type=jnp.float32
        )
        attended = (attended / denominator).astype(jnp.bfloat16)
        for h in range(rows // window):
            out_ref[n * window : (n + 1) * window, h * head_dim : (h + 1) * head_dim] = attended[
                h * window : (h + 1) * window
            ]


def attend(table, visible, queries, drafts, arrived, window, per_step=2):
    requests, rows, head_dim = queries.shape
    slots = arrived.shape[0]
    return pl.pallas_call(
        functools.partial(attend_kernel, per_step),
        out_shape=jax.ShapeDtypeStruct((requests * window, rows // window * head_dim), jnp.bfloat16),
        grid_spec=pltpu.PrefetchScalarGridSpec(
            num_scalar_prefetch=2,
            grid=(requests // per_step,),
            in_specs=[
                pl.BlockSpec((per_step, rows, head_dim), lambda i, *_: (i, 0, 0)),
                pl.BlockSpec((per_step,) + drafts.shape[1:], lambda i, *_: (i, 0, 0)),
                pl.BlockSpec(memory_space=pl.ANY),
            ],
            out_specs=pl.BlockSpec(
                (per_step * window, rows // window * head_dim), lambda i, *_: (i, 0)
            ),
            scratch_shapes=[
                pltpu.VMEM((slots + 1,) + arrived.shape[1:], arrived.dtype),
                pltpu.SemaphoreType.DMA((load_pieces,)),
            ],
        ),
        cost_estimate=pl.CostEstimate(flops=1 << 30, bytes_accessed=10 << 20, transcendentals=1 << 21),
        name="attend",
    )(table, visible, queries, drafts, arrived)


def on_device(
    queries,
    draft_kv,
    kv_pool,
    block_dest,
    block_table,
    context_len,
    draft_len,
    accept_mask,
    out_weight,
    residual,
    norm_gain,
):
    rank_count = lax.axis_size("dp")
    pool_count = kv_pool.shape[0]
    capacity = 2 * pool_count // rank_count
    requests, heads_local, window, head_dim = queries.shape
    block_len = kv_pool.shape[3]
    pool = kv_pool.reshape(pool_count, 2 * block_len, head_dim)
    outgoing = pack_blocks(block_dest, pool, rank_count, capacity)
    arrived = lax.all_to_all(outgoing, "dp", split_axis=0, concat_axis=0, tiled=True)
    kept_count = jnp.sum(jnp.cumprod(accept_mask, axis=1, dtype=jnp.int32), axis=1, dtype=jnp.int32)
    visible = context_len - window + kept_count
    token_rows = attend(
        block_table.reshape(-1),
        visible,
        queries.reshape(requests, heads_local * window, head_dim),
        draft_kv.reshape(requests, 2 * window, head_dim),
        arrived,
        window,
    )
    partial_value = jnp.dot(token_rows, out_weight, preferred_element_type=jnp.float32)
    column_count = norm_gain.shape[0]
    column_start = lax.axis_index("mp") * column_count
    live_rows = (jnp.arange(window, dtype=jnp.int32)[None, :] < draft_len[:, None]).reshape(
        requests * window
    )
    share = lax.psum_scatter(
        partial_value.astype(jnp.bfloat16), "mp", scatter_dimension=1, tiled=True
    ).astype(jnp.float32)
    local_residual = lax.dynamic_slice_in_dim(residual, column_start, column_count, 1)
    local_hidden = local_residual.astype(jnp.float32) + share
    squares = over_copies(jnp.sum(local_hidden * local_hidden, axis=1), "mp")
    mean_square = (squares / (column_count * lax.axis_size("mp")))[:, None]
    normed = local_hidden * lax.rsqrt(mean_square + norm_epsilon) * norm_gain[None, :]
    return jnp.where(live_rows[:, None], normed, 0.0).astype(jnp.bfloat16)


def solution(mesh):
    return jax.shard_map(
        on_device,
        mesh=mesh,
        in_specs=(
            P("dp", "mp", None, None),
            P("dp", None, "mp", None, None),
            P("dp", None, "mp", None, None),
            P("dp"),
            P("dp", None),
            P("dp"),
            P("dp"),
            P("dp", None),
            P("mp", None),
            P("dp", None),
            P("mp"),
        ),
        out_specs=P("dp", "mp"),
        check_vma=False,
    )
```

time: 447 us -> 307 us (0.69)
  local copies, waits for them, and re-layouts: 86.9 us -> 1.48 us
  matrix products: 66.8 us -> 10.2 us
  other arithmetic: 30.8 us -> 4.6 us
  Pallas kernels: 0 us -> 25.4 us
    dot_general x4 -> x0, matrix products: 60.7 us -> none  [the longest x1 28.7 us: on_device(): jnp.einsum('rkgwbp,rbkpd->rkgwd', cached_prob, cached_values, preferred_e...]
    scatter x1 -> x0, local copies, waits for them, and re-layouts: 58.8 us -> none  [on_device(): outgoing = jnp.zeros((rank_count * capacity,) + kv_pool.shape[1:], jnp.bf...]
    pallas_call x0 -> x2, Pallas kernels: none -> 25.4 us  [the longest x1 19.1 us: attend(): pl.pallas_call(functools.partial(attend_kernel, per_step), out_shape=jax....]
    reduce_sum x3 -> x0, other arithmetic: 23.2 us -> none  [the longest x2 22.4 us: on_device(): denominator = jnp.sum(cached_exp, axis=4) + jnp.sum(draft_exp, axis=4)]
    gather x2 -> x0, local copies, waits for them, and re-layouts: 21.3 us -> none  [on_device(): gathered = arrived[block_table]]
where the time goes in v1:
time: 307 us; the launch traced here: 306 us
  waiting for transfers between devices  232 us (76%)
  Pallas kernels  25.4 us (8%)
  starting transfers between devices  19.2 us (6%)
  between operations  13.5 us (4%)
  matrix products  10.2 us (3%)
  other arithmetic  4.6 us (1%)
    all_to_all x1, waiting for transfers between devices, on_device(): lax.all_to_all(outgoing, 'dp', split_axis=0, concat_axis=0, tiled=True)  187 us
    reduce_scatter x1, waiting for transfers between devices, on_device(): lax.psum_scatter(partial_value.astype(jnp.bfloat16), 'mp', scatter_dimens...  40.5 us
    pallas_call x1, Pallas kernels, attend(): pl.pallas_call(functools.partial(attend_kernel, per_step), out_shape=jax....  19.1 us
    all_to_all x1, starting transfers between devices, on_device(): lax.all_to_all(outgoing, 'dp', split_axis=0, concat_axis=0, tiled=True)  12.5 us
    dot_general x1, matrix products, on_device(): jnp.dot(token_rows, out_weight, preferred_element_type=jnp.float32)  10.2 us
    all_to_all x1, starting transfers between devices, from_everyone(): lax.all_to_all(jnp.broadcast_to(array[None], (length, *array.shape)), axi...  6.61 us
    pallas_call x1, Pallas kernels, pack_blocks(): pl.pallas_call(functools.partial(pack_kernel, rank_count, capacity), out_...  6.31 us
  transfers between devices with their start and end apart: 3, of which 3 were waited for; matrix products, arithmetic and copies ran while one was open for 1% of the time, Pallas kernels for 0%

profile of v1, /device:TPU:1, one launch (start us, length us, event | category | flops | bytes accessed | tf_op | source)
XLA Modules:
  0.0 305.9 jit_solution(18335275386921834413)
XLA Ops:
  6.5 6.3 %pack_blocks.1 = bf16[1024,32,128]{2,1,0:T(8,128)(2,1)} custom-call(s32[512]{0:T(512)} %dest_ref.1, bf16[512,32,128]{2,1,0:T(8,128)(2,1)} %bitcast.5), custom_call_target="tpu_custom_call" | custom-call | bytes 8388608 | tf_op jit(solution)/shard_map/pack_blocks/pallas_call | solution.py:73
  12.9 0.0 copy-start.1
  12.9 0.0 copy-start
  12.9 12.5 %all-to-all-start = ((bf16[1024,32,128]{2,1,0:T(8,128)(2,1)}), bf16[1024,32,128]{2,1,0:T(8,128)(2,1)}, u32[]{:S(2)}, u32[]{:S(2)}) async-start(bf16[1024,32,128]{2,1,0:T(8,128)(2,1)} %pack_blocks.1), calls=%async_computation | async-start | bytes 16777216 | tf_op jit(solution)/shard_map/all_to_all | solution.py:202
  25.4 0.0 reduce-scatter.2.cloned.1.call-start
  25.5 0.1 copy.15
  25.5 0.7 reshape.41.table_ref
  26.2 0.2 reduce_window.9
  26.4 0.1 reduce_sum.27
  26.5 0.5 add_add_fusion.visible_ref
  27.0 186.6 %all-to-all-done.arrived_ref = bf16[1024,32,128]{2,1,0:T(8,128)(2,1)} async-done(((bf16[1024,32,128]{2,1,0:T(8,128)(2,1)}), bf16[1024,32,128]{2,1,0:T(8,128)(2,1)}, u32[]{:S(2)}, u32[]{:S(2)}) %all-to-all-start) | async-done | bytes 8388640 | tf_op jit(solution)/shard_map/all_to_all | solution.py:202
  213.6 19.1 %attend.1 = bf16[512,1024]{1,0:T(8,128)(2,1)} custom-call(s32[1024]{0:T(1024)} %reshape.41.table_ref, s32[32]{0:T(128)} %add_add_fusion.visible_ref, bf16[32,128,128]{2,1,0:T(8,128)(2,1)} %bitcast.6, bf16[32,32,128]{2,1,0:T(8,128)(2,1)} %bitcast.7, bf16[1024,32,128]{2,1,0:T(8,128)(2,1)} %all-to-all-done.arrived_ref), custom_call_target="tpu_custom_call" | custom-call | flops 1073741824 | bytes 10485760 | tf_op jit(solution)/shard_map/attend/pallas_call | solution.py:158
  232.7 0.0 copy-start.3
  232.7 0.0 copy-start.2
  232.7 10.2 %convolution_convert_fusion = bf16[512,4096]{1,0:T(8,128)(2,1)} fusion(bf16[512,1024]{1,0:T(8,128)(2,1)} %attend.1, bf16[1024,4096]{1,0:T(8,128)(2,1)} %param.19), kind=kOutput, calls=%fused_computation | convolution fusion | flops 4297064448 | bytes 13631488 | tf_op jit(solution)/shard_map/dot_general | solution.py:213
  242.9 0.0 reduce-scatter.2.cloned.1.call-update
  242.9 40.5 %reduce-scatter.2.cloned.1.call-done = bf16[512,512]{1,0:T(8,128)(2,1)} async-done(((bf16[512,4096]{1,0:T(8,128)(2,1)}), bf16[512,512]{1,0:T(8,128)(2,1)}) %reduce-scatter.2.cloned.1.call-update) | async-done | bytes 524304 | tf_op jit(solution)/shard_map/reduce_scatter | solution.py:219
  283.4 1.4 multiply_reduce_fusion
  284.9 0.6 broadcast_in_dim.11
  285.5 6.6 %all-to-all-start.1 = ((f32[8,1,512]{2,1,0:T(1,128)}), f32[8,1,512]{2,1,0:T(1,128)S(1)}, u32[]{:S(2)}, u32[]{:S(2)}) async-start(f32[8,1,512]{2,1,0:T(1,128)} %broadcast_in_dim.11), calls=%async_computation.2 | async-start | bytes 32768 | tf_op jit(solution)/shard_map/all_to_all | solution.py:18
  292.1 0.1 iota_compare_fusion
  292.2 0.1 lt.26
  292.3 4.5 %all-to-all-done.1 = f32[8,1,512]{2,1,0:T(1,128)S(1)} async-done(((f32[8,1,512]{2,1,0:T(1,128)}), f32[8,1,512]{2,1,0:T(1,128)S(1)}, u32[]{:S(2)}, u32[]{:S(2)}) %all-to-all-start.1) | async-done | bytes 16416 | tf_op jit(solution)/shard_map/all_to_all | solution.py:18
  296.8 2.3 select_convert_fusion
  (8 shorter events, 0.1 us)
Async XLA Ops:
  12.9 12.6 %copy-start.1 = (s32[32,16]{0,1:T(8,128)S(1)}, s32[32,16]{0,1:T(8,128)}, u32[]{:S(2)}) copy-start(s32[32,16]{0,1:T(8,128)} %param.18) | copy-start | bytes 6148
  12.9 12.7 %copy-start = (s32[32,32]{1,0:T(8,128)S(1)}, s32[32,32]{1,0:T(8,128)}, u32[]{:S(2)}) copy-start(s32[32,32]{1,0:T(8,128)} %param.15) | copy-start | bytes 12292
  12.9 13.6 %copy-start.4 = (s32[32]{0:T(128)S(1)}, s32[32]{0:T(128)}, u32[]{:S(2)}) copy-start(s32[32]{0:T(128)} %param.16) | copy-start | bytes 388
  12.9 200.7 %all-to-all-start = ((bf16[1024,32,128]{2,1,0:T(8,128)(2,1)}), bf16[1024,32,128]{2,1,0:T(8,128)(2,1)}, u32[]{:S(2)}, u32[]{:S(2)}) async-start(bf16[1024,32,128]{2,1,0:T(8,128)(2,1)} %pack_blocks.1), calls=%async_computation | async-start | bytes 16777216 | tf_op jit(solution)/shard_map/all_to_all | solution.py:202
  25.4 258.0 %reduce-scatter.2.cloned.1.call-start = ((), (), s32[]{:S(2)}) async-start(), calls=%async_computation.3 | async-start | bytes 4718592 | tf_op jit(solution)/shard_map/reduce_scatter | solution.py:219
  232.7 59.4 %copy-start.3 = (s32[32]{0:T(128)S(1)}, s32[32]{0:T(128)}, u32[]{:S(2)}) copy-start(s32[32]{0:T(128)} %param.17) | copy-start | bytes 388
  232.7 64.1 %copy-start.2 = (f32[512]{0:T(512)S(1)}, f32[512]{0:T(512)}, u32[]{:S(2)}) copy-start(f32[512]{0:T(512)} %param.21) | copy-start | bytes 6148
  285.5 11.3 %all-to-all-start.1 = ((f32[8,1,512]{2,1,0:T(1,128)}), f32[8,1,512]{2,1,0:T(1,128)S(1)}, u32[]{:S(2)}, u32[]{:S(2)}) async-start(f32[8,1,512]{2,1,0:T(1,128)} %broadcast_in_dim.11), calls=%async_computation.2 | async-start | bytes 32768 | tf_op jit(solution)/shard_map/all_to_all | solution.py:18
Sparse Core Ops, SparseCore 0:
  243.0 40.3 reduce-scatter.1

commit v2 on v1

--- a/solution.py
+++ b/solution.py
@@ -179,6 +179,42 @@
     )(table, visible, queries, drafts, arrived)
 
 
+def project(token_rows, out_weight, column_count):
+    size = lax.axis_size("mp")
+    chips = size // 2
+    place = lax.axis_index("mp")
+    core = place % 2
+    swap = [(i, i ^ 1) for i in range(size)]
+    right = [(i, (i + 2) % size) for i in range(size)]
+    left = [(i, (i - 2) % size) for i in range(size)]
+
+    def columns(k, c):
+        chip = (place // 2 + k) % chips
+        return lax.dynamic_slice_in_dim(out_weight, (chip * 2 + c) * column_count, column_count, 1)
+
+    own_weight = [columns(k, core) for k in range(chips)]
+    given = jnp.concatenate([columns(k, 1 - core) for k in range(chips)], axis=0)
+    their_weight = jnp.split(lax.ppermute(given, "mp", swap), chips, axis=0)
+    theirs = lax.ppermute(token_rows, "mp", swap)
+
+    def partial(k):
+        own = jnp.dot(token_rows, own_weight[k], preferred_element_type=jnp.float32)
+        return own + jnp.dot(theirs, their_weight[k], preferred_element_type=jnp.float32)
+
+    half = column_count // 2
+    far = partial(2).astype(jnp.bfloat16)
+    from_left = lax.ppermute(far[:, :half], "mp", right)
+    from_right = lax.ppermute(far[:, half:], "mp", left)
+    ahead = partial(1)
+    behind = partial(3)
+    home = partial(0)
+    ahead = jnp.concatenate([ahead[:, :half] + from_left.astype(jnp.float32), ahead[:, half:]], axis=1)
+    behind = jnp.concatenate([behind[:, :half], behind[:, half:] + from_right.astype(jnp.float32)], axis=1)
+    from_left = lax.ppermute(ahead.astype(jnp.bfloat16), "mp", right)
+    from_right = lax.ppermute(behind.astype(jnp.bfloat16), "mp", left)
+    return home + from_left.astype(jnp.float32) + from_right.astype(jnp.float32)
+
+
 def on_device(
     queries,
     draft_kv,
@@ -210,16 +246,13 @@
         arrived,
         window,
     )
-    partial_value = jnp.dot(token_rows, out_weight, preferred_element_type=jnp.float32)
     column_count = norm_gain.shape[0]
-    column_start = lax.axis_index("mp") * column_count
+    place = lax.axis_index("mp")
     live_rows = (jnp.arange(window, dtype=jnp.int32)[None, :] < draft_len[:, None]).reshape(
         requests * window
     )
-    share = lax.psum_scatter(
-        partial_value.astype(jnp.bfloat16), "mp", scatter_dimension=1, tiled=True
-    ).astype(jnp.float32)
-    local_residual = lax.dynamic_slice_in_dim(residual, column_start, column_count, 1)
+    share = project(token_rows, out_weight, column_count)
+    local_residual = lax.dynamic_slice_in_dim(residual, place * column_count, column_count, 1)
     local_hidden = local_residual.astype(jnp.float32) + share
     squares = over_copies(jnp.sum(local_hidden * local_hidden, axis=1), "mp")
     mean_square = (squares / (column_count * lax.axis_size("mp")))[:, None]

time: 307 us -> 284 us (0.925)
  waiting for transfers between devices: 232 us -> 200 us
  between operations: 13.5 us -> 0.37 us
  matrix products: 10.2 us -> 17.6 us
  starting transfers between devices: 19.2 us -> 26.2 us
  local copies, waits for them, and re-layouts: 1.48 us -> 6.36 us
    reduce_scatter x1 -> x0, waiting for transfers between devices: 40.5 us -> none  [on_device(): lax.psum_scatter(partial_value.astype(jnp.bfloat16), 'mp', scatter_dimens...]
    ppermute x0 -> x6, waiting for transfers between devices: none -> 15.1 us  [the longest x1 7.3 us: project(): from_left = lax.ppermute(ahead.astype(jnp.bfloat16), 'mp', right)]
    ppermute x0 -> x6, starting transfers between devices: none -> 8.96 us  [the longest x1 3.49 us: project(): from_right = lax.ppermute(behind.astype(jnp.bfloat16), 'mp', left)]
    dot_general x1 -> x8, matrix products: 10.2 us -> 17.6 us  [the longest x4 9.19 us: partial(): own = jnp.dot(token_rows, own_weight[k], preferred_element_type=jnp.float32)]
    all_to_all x1, waiting for transfers between devices: 187 us -> 181 us  [on_device(): lax.all_to_all(outgoing, 'dp', split_axis=0, concat_axis=0, tiled=True)]
    dynamic_slice x0 -> x2, local copies, waits for them, and re-layouts: none -> 3.56 us  [the longest x1 2.48 us: columns(): lax.dynamic_slice_in_dim(out_weight, (chip * 2 + c) * column_count, colum...]
  transfers between devices with their start and end apart: 3 -> 8, of which waited for: 3 -> 6; matrix products, arithmetic and copies ran while one was open for 1% -> 8% of each run, Pallas kernels for 0% -> 7%
where the time goes in v2:
time: 284 us; the launch traced here: 280 us
  waiting for transfers between devices  200 us (70%)
  starting transfers between devices  26.2 us (9%)
  Pallas kernels  25.7 us (9%)
  matrix products  17.6 us (6%)
  local copies, waits for them, and re-layouts  6.36 us (2%)
  other arithmetic  3.56 us (1%)
    all_to_all x1, waiting for transfers between devices, on_device(): lax.all_to_all(outgoing, 'dp', split_axis=0, concat_axis=0, tiled=True)  181 us
    pallas_call x1, Pallas kernels, attend(): pl.pallas_call(functools.partial(attend_kernel, per_step), out_shape=jax....  19.1 us
    all_to_all x1, starting transfers between devices, on_device(): lax.all_to_all(outgoing, 'dp', split_axis=0, concat_axis=0, tiled=True)  12 us
    dot_general x4, matrix products, partial(): own = jnp.dot(token_rows, own_weight[k], preferred_element_type=jnp.float32)  9.19 us
    dot_general x4, matrix products, partial(): jnp.dot(theirs, their_weight[k], preferred_element_type=jnp.float32)  8.43 us
    ppermute x1, waiting for transfers between devices, project(): from_left = lax.ppermute(ahead.astype(jnp.bfloat16), 'mp', right)  7.3 us
    pallas_call x1, Pallas kernels, pack_blocks(): pl.pallas_call(functools.partial(pack_kernel, rank_count, capacity), out_...  6.58 us
  transfers between devices with their start and end apart: 8, of which 6 were waited for; matrix products, arithmetic and copies ran while one was open for 8% of the time, Pallas kernels for 7%

profile of v2, /device:TPU:1, one launch (start us, length us, event | category | flops | bytes accessed | tf_op | source)
XLA Modules:
  0.0 280.2 jit_solution(1360882172942577965)
XLA Ops:
  0.0 6.6 %pack_blocks.1 = bf16[1024,32,128]{2,1,0:T(8,128)(2,1)} custom-call(s32[512]{0:T(512)} %dest_ref.1, bf16[512,32,128]{2,1,0:T(8,128)(2,1)} %bitcast.11), custom_call_target="tpu_custom_call" | custom-call | bytes 8388608 | tf_op jit(solution)/shard_map/pack_blocks/pallas_call | solution.py:73
  6.6 12.0 %all-to-all-start = ((bf16[1024,32,128]{2,1,0:T(8,128)(2,1)}), bf16[1024,32,128]{2,1,0:T(8,128)(2,1)}, u32[]{:S(2)}, u32[]{:S(2)}) async-start(bf16[1024,32,128]{2,1,0:T(8,128)(2,1)} %pack_blocks.1), calls=%async_computation | async-start | bytes 16777216 | tf_op jit(solution)/shard_map/all_to_all | solution.py:238
  18.7 2.5 constant_dynamic-slice_fusion.3
  21.2 2.2 pad_maximum_fusion
  26.0 180.8 %all-to-all-done.arrived_ref = bf16[1024,32,128]{2,1,0:T(8,128)(2,1)} async-done(((bf16[1024,32,128]{2,1,0:T(8,128)(2,1)}), bf16[1024,32,128]{2,1,0:T(8,128)(2,1)}, u32[]{:S(2)}, u32[]{:S(2)}) %all-to-all-start) | async-done | bytes 8388640 | tf_op jit(solution)/shard_map/all_to_all | solution.py:238
  206.7 19.1 %attend.1 = bf16[512,1024]{1,0:T(8,128)(2,1)} custom-call(s32[1024]{0:T(1024)} %reshape.41.table_ref, s32[32]{0:T(128)} %add_add_fusion.visible_ref, bf16[32,128,128]{2,1,0:T(8,128)(2,1)} %bitcast.12, bf16[32,32,128]{2,1,0:T(8,128)(2,1)} %bitcast.13, bf16[1024,32,128]{2,1,0:T(8,128)(2,1)} %all-to-all-done.arrived_ref), custom_call_target="tpu_custom_call" | custom-call | flops 1073741824 | bytes 10485760 | tf_op jit(solution)/shard_map/attend/pallas_call | solution.py:158
  225.9 1.6 collective-permute-start
  227.5 2.3 fusion.8
  229.8 2.3 fusion.10
  232.1 2.3 fusion.12
  234.4 2.0 fusion.3
  236.4 2.6 collective-permute-start.4
  239.0 2.0 convolution_add_fusion
  241.0 2.0 convolution_add_fusion.2
  243.2 1.4 collective-permute-done.4
  244.7 3.5 %collective-permute-start.5 = (bf16[512,512]{0,1:T(8,128)(2,1)S(1)}, bf16[512,512]{0,1:T(8,128)(2,1)}, u32[]{:S(2)}, u32[]{:S(2)}) collective-permute-start(bf16[512,512]{0,1:T(8,128)(2,1)S(1)} %pad_maximum_fusion.2), channel_id=1, source_target_pairs={{0,6},{1,7},{2,0},{3,1},{4,2},{5,3},{6,4},{7,5},{8,14},{9,15},{10,... | collective-permute-start | bytes 1572872 | tf_op jit(solution)/shard_map/ppermute | solution.py:214
  248.2 3.7 %collective-permute-done.2 = bf16[512,256]{0,1:T(8,128)(2,1)S(1)} collective-permute-done((bf16[512,256]{0,1:T(8,128)(2,1)S(1)}, bf16[512,256]{0,1:T(8,128)(2,1)S(1)}, u32[]{:S(2)}, u32[]{:S(2)}) %collective-permute-start.2) | collective-permute-done | bytes 262176 | tf_op jit(solution)/shard_map/ppermute | solution.py:206
  252.3 1.1 constant_dynamic-slice_fusion.4
  253.6 2.3 fusion.14
  255.9 2.7 collective-permute-done.5
  258.6 7.3 %collective-permute-done.3 = bf16[512,512]{0,1:T(8,128)(2,1)} collective-permute-done((bf16[512,512]{0,1:T(8,128)(2,1)S(1)}, bf16[512,512]{0,1:T(8,128)(2,1)}, u32[]{:S(2)}, u32[]{:S(2)}) %collective-permute-start.3) | collective-permute-done | bytes 524320 | tf_op jit(solution)/shard_map/ppermute | solution.py:213
  265.9 2.5 multiply_reduce_fusion
  269.0 5.3 %all-to-all-start.1 = ((f32[8,1,512]{2,1,0:T(1,128)}), f32[8,1,512]{2,1,0:T(1,128)S(1)}, u32[]{:S(2)}, u32[]{:S(2)}) async-start(f32[8,1,512]{2,1,0:T(1,128)} %broadcast_in_dim.11), calls=%async_computation.1 | async-start | bytes 32768 | tf_op jit(solution)/shard_map/all_to_all | solution.py:18
  274.4 4.5 %all-to-all-done.1 = f32[8,1,512]{2,1,0:T(1,128)S(1)} async-done(((f32[8,1,512]{2,1,0:T(1,128)}), f32[8,1,512]{2,1,0:T(1,128)S(1)}, u32[]{:S(2)}, u32[]{:S(2)}) %all-to-all-start.1) | async-done | bytes 16416 | tf_op jit(solution)/shard_map/all_to_all | solution.py:18
  (35 shorter events, 5.5 us)
Async XLA Ops:
  6.6 200.2 %all-to-all-start = ((bf16[1024,32,128]{2,1,0:T(8,128)(2,1)}), bf16[1024,32,128]{2,1,0:T(8,128)(2,1)}, u32[]{:S(2)}, u32[]{:S(2)}) async-start(bf16[1024,32,128]{2,1,0:T(8,128)(2,1)} %pack_blocks.1), calls=%async_computation | async-start | bytes 16777216 | tf_op jit(solution)/shard_map/all_to_all | solution.py:238
  18.7 5.7 %copy-start = (s32[32,32]{1,0:T(8,128)S(1)}, s32[32,32]{1,0:T(8,128)}, u32[]{:S(2)}) copy-start(s32[32,32]{1,0:T(8,128)} %param.15) | copy-start | bytes 12292
  18.7 6.3 %copy-start.1 = (s32[32,16]{0,1:T(8,128)S(1)}, s32[32,16]{0,1:T(8,128)}, u32[]{:S(2)}) copy-start(s32[32,16]{0,1:T(8,128)} %param.18) | copy-start | bytes 6148
  18.7 6.7 %copy-start.4 = (s32[32]{0:T(128)S(1)}, s32[32]{0:T(128)}, u32[]{:S(2)}) copy-start(s32[32]{0:T(128)} %param.16) | copy-start | bytes 388
  23.4 211.0 %collective-permute-start.1 = (bf16[4096,512]{1,0:T(8,128)(2,1)}, bf16[4096,512]{1,0:T(8,128)(2,1)}, u32[]{:S(2)}, u32[]{:S(2)}) collective-permute-start(bf16[4096,512]{1,0:T(8,128)(2,1)} %pad_maximum_fusion), channel_id=1, source_target_pairs={{0,1},{1,0},{2,3},{3,2},{4,5},{5,4},{6,7},{7,6},{8,9},{9,8},{10,11... | collective-permute-start | bytes 12582920 | tf_op jit(solution)/shard_map/ppermute | solution.py:197
  225.9 8.5 %collective-permute-start = (bf16[512,1024]{1,0:T(8,128)(2,1)}, bf16[512,1024]{1,0:T(8,128)(2,1)S(1)}, u32[]{:S(2)}, u32[]{:S(2)}) collective-permute-start(bf16[512,1024]{1,0:T(8,128)(2,1)} %attend.1), channel_id=1, source_target_pairs={{0,1},{1,0},{2,3},{3,2},{4,5},{5,4},{6,7},{7,6},{8,9},{9,8},{10,11... | collective-permute-start | bytes 3145736 | tf_op jit(solution)/shard_map/ppermute | solution.py:198
  236.4 8.2 %collective-permute-start.4 = (bf16[512,256]{0,1:T(8,128)(2,1)S(1)}, bf16[512,256]{0,1:T(8,128)(2,1)S(1)}, u32[]{:S(2)}, u32[]{:S(2)}) collective-permute-start(bf16[512,256]{0,1:T(8,128)(2,1)S(1)} %get-tuple-element.10), channel_id=1, source_target_pairs={{0,6},{1,7},{2,0},{3,1},{4,2},{5,3},{6,4},{7,5},{8,14},{9,15},{10,... | collective-permute-start | bytes 786440 | tf_op jit(solution)/shard_map/ppermute | solution.py:207
  243.0 31.3 %copy-start.3 = (s32[32]{0:T(128)S(1)}, s32[32]{0:T(128)}, u32[]{:S(2)}) copy-start(s32[32]{0:T(128)} %param.17) | copy-start | bytes 388
  243.0 36.0 %copy-start.2 = (f32[512]{0:T(512)S(1)}, f32[512]{0:T(512)}, u32[]{:S(2)}) copy-start(f32[512]{0:T(512)} %param.21) | copy-start | bytes 6148
  243.1 8.8 %collective-permute-start.2 = (bf16[512,256]{0,1:T(8,128)(2,1)S(1)}, bf16[512,256]{0,1:T(8,128)(2,1)S(1)}, u32[]{:S(2)}, u32[]{:S(2)}) collective-permute-start(bf16[512,256]{0,1:T(8,128)(2,1)S(1)} %get-tuple-element.9), channel_id=1, source_target_pairs={{0,2},{1,3},{2,4},{3,5},{4,6},{5,7},{6,0},{7,1},{8,10},{9,11},{10,... | collective-permute-start | bytes 786440 | tf_op jit(solution)/shard_map/ppermute | solution.py:206
  244.7 13.9 %collective-permute-start.5 = (bf16[512,512]{0,1:T(8,128)(2,1)S(1)}, bf16[512,512]{0,1:T(8,128)(2,1)}, u32[]{:S(2)}, u32[]{:S(2)}) collective-permute-start(bf16[512,512]{0,1:T(8,128)(2,1)S(1)} %pad_maximum_fusion.2), channel_id=1, source_target_pairs={{0,6},{1,7},{2,0},{3,1},{4,2},{5,3},{6,4},{7,5},{8,14},{9,15},{10,... | collective-permute-start | bytes 1572872 | tf_op jit(solution)/shard_map/ppermute | solution.py:214
  252.0 13.9 %collective-permute-start.3 = (bf16[512,512]{0,1:T(8,128)(2,1)S(1)}, bf16[512,512]{0,1:T(8,128)(2,1)}, u32[]{:S(2)}, u32[]{:S(2)}) collective-permute-start(bf16[512,512]{0,1:T(8,128)(2,1)S(1)} %pad_maximum_fusion.1), channel_id=1, source_target_pairs={{0,2},{1,3},{2,4},{3,5},{4,6},{5,7},{6,0},{7,1},{8,10},{9,11},{10,... | collective-permute-start | bytes 1572872 | tf_op jit(solution)/shard_map/ppermute | solution.py:213
  269.0 9.9 %all-to-all-start.1 = ((f32[8,1,512]{2,1,0:T(1,128)}), f32[8,1,512]{2,1,0:T(1,128)S(1)}, u32[]{:S(2)}, u32[]{:S(2)}) async-start(f32[8,1,512]{2,1,0:T(1,128)} %broadcast_in_dim.11), calls=%async_computation.1 | async-start | bytes 32768 | tf_op jit(solution)/shard_map/all_to_all | solution.py:18

commit v3 on v2

v3 whole, which is shorter than its diff:
```python
import functools
import math

import jax
import jax.numpy as jnp
from jax import lax
from jax.experimental import pallas as pl
from jax.experimental.pallas import tpu as pltpu
from jax.sharding import PartitionSpec as P


masked_score = -1e30
norm_epsilon = 1e-05
load_pieces = 2
ring_len = 8
room = (168, 168, 124, 52)


def over(array, power):
    return lax.shift_right_arithmetic(array, jnp.int32(power.bit_length() - 1))


def rest(array, power):
    return jnp.bitwise_and(array, power - 1)


def from_everyone(array, axis):
    length = lax.axis_size(axis)
    return lax.all_to_all(
        jnp.broadcast_to(array[None], (length, *array.shape)), axis, 0, 0, tiled=True
    )


def over_copies(array, axis):
    everything = from_everyone(array, axis)
    return jnp.sum(everything, axis=0)


def pack_kernel(halved, kinds, dest_ref, start_ref, pool_ref, *refs):
    outs, (staged, used, sem, out_sem) = refs[:-4], refs[-4:]
    blocks = pool_ref.shape[0]
    slots = staged.shape[0] - blocks

    def clear(d, carry):
        used[d] = 0
        return carry

    lax.fori_loop(0, kinds + 1, clear, 0)

    def place(b, carry):
        d = dest_ref[b]
        k = used[d]
        used[d] = k + 1
        slot = start_ref[2 * d + (k & 1)] + jnp.where(halved(d), k >> 1, k)
        slot = jnp.where(d < kinds, jnp.minimum(slot, slots - 1), slots + b)
        pltpu.make_async_copy(pool_ref.at[b], staged.at[slot], sem).start()
        return carry

    lax.fori_loop(0, blocks, place, 0, unroll=4 if len(outs) > 1 else 1)
    pltpu.make_async_copy(pool_ref, staged.at[pl.ds(0, blocks)], sem).wait()
    copies, at = [], 0
    for n, out in enumerate(outs):
        rows = pl.ds(at, out.shape[0])
        copies.append(pltpu.make_async_copy(staged.at[rows], out, out_sem.at[n]))
        at += out.shape[0]
    for copy in copies:
        copy.start()
    for copy in copies:
        copy.wait()


def pack_blocks(dest, start, pool, sizes, halved):
    kinds = start.shape[0] // 2 - 1
    return pl.pallas_call(
        functools.partial(pack_kernel, halved, kinds),
        out_shape=[jax.ShapeDtypeStruct((n,) + pool.shape[1:], pool.dtype) for n in sizes],
        in_specs=[
            pl.BlockSpec(memory_space=pltpu.SMEM),
            pl.BlockSpec(memory_space=pltpu.SMEM),
            pl.BlockSpec(memory_space=pl.ANY),
        ],
        out_specs=[pl.BlockSpec(memory_space=pl.ANY)] * len(sizes),
        scratch_shapes=[
            pltpu.VMEM((sum(sizes) + pool.shape[0],) + pool.shape[1:], pool.dtype),
            pltpu.SMEM((kinds + 1,), jnp.int32),
            pltpu.SemaphoreType.DMA,
            pltpu.SemaphoreType.DMA((len(sizes),)),
        ],
        cost_estimate=pl.CostEstimate(flops=1 << 28, bytes_accessed=1 << 23, transcendentals=0),
        name="pack_blocks",
    )(dest, start, pool)


def pick_kernel(plans, offset_ref, *refs):
    sources, outs, sem = refs[: -len(plans) - 1], refs[-len(plans) - 1 : -1], refs[-1]
    copies = []
    for plan, out in zip(plans, outs):
        at = 0
        for source, (kind, number), length in plan:
            start = offset_ref[number] if kind == "offset" else number
            copies.append(
                pltpu.make_async_copy(
                    sources[source].at[pl.ds(start, length)],
                    out.at[pl.ds(at, length)],
                    sem.at[len(copies)],
                )
            )
            at += length
    for copy in copies:
        copy.start()
    for copy in copies:
        copy.wait()


def pick(offsets, sources, plans):
    shape = sources[0].shape[1:]
    sizes = [sum(length for _, _, length in plan) for plan in plans]
    return pl.pallas_call(
        functools.partial(pick_kernel, plans),
        out_shape=[jax.ShapeDtypeStruct((n,) + shape, sources[0].dtype) for n in sizes],
        in_specs=[pl.BlockSpec(memory_space=pltpu.SMEM)]
        + [pl.BlockSpec(memory_space=pl.ANY)] * len(sources),
        out_specs=[pl.BlockSpec(memory_space=pltpu.VMEM)] * len(plans),
        scratch_shapes=[pltpu.SemaphoreType.DMA((sum(len(plan) for plan in plans),))],
        cost_estimate=pl.CostEstimate(flops=1 << 20, bytes_accessed=4 << 20, transcendentals=0),
        name="pick",
    )(offsets, *sources)


def attend_kernel(per_step, plan, table_ref, visible_ref, offset_ref, queries_ref, draft_ref, *refs):
    sources, (out_ref, cache, load_sem) = refs[:-3], refs[-3:]
    slots = cache.shape[0] - 1
    step = pl.program_id(0)
    width = table_ref.shape[0] // visible_ref.shape[0]
    block_len = cache.shape[1] // 2
    rows, head_dim = queries_ref.shape[1:]
    window = out_ref.shape[0] // per_step
    log_scale = math.log2(math.e) / math.sqrt(head_dim)

    @pl.when(step == 0)
    def _():
        copies, at = [], 0
        for source, (kind, number), length in plan:
            start = offset_ref[number] if kind == "offset" else number
            copies.append(
                pltpu.make_async_copy(
                    sources[source].at[pl.ds(start, length)],
                    cache.at[pl.ds(at, length)],
                    load_sem.at[len(copies)],
                )
            )
            at += length
        for copy in copies:
            copy.start()
        cache[slots] = jnp.zeros_like(cache[slots])
        for copy in copies:
            copy.wait()

    positions = lax.broadcasted_iota(jnp.int32, (rows, width * block_len), 1)
    query_place = rest(lax.broadcasted_iota(jnp.int32, (rows, window), 0), window)
    causal = lax.broadcasted_iota(jnp.int32, (rows, window), 1) <= query_place
    over_last = (((1,), (1,)), ((), ()))
    for n in range(per_step):
        request = step * per_step + n
        visible = visible_ref[request]
        places = [
            jnp.where(e * block_len < visible, table_ref[request * width + e], slots)
            for e in range(width)
        ]
        keys = jnp.concatenate([cache[s, :block_len, :] for s in places], axis=0)
        values = jnp.concatenate([cache[s, block_len:, :] for s in places], axis=0)
        query = queries_ref[n]
        cached = lax.dot_general(query, keys, over_last, preferred_element_type=jnp.float32)
        cached = jnp.where(positions < visible, cached, masked_score)
        drafts = lax.dot_general(
            query, draft_ref[n, :window, :], over_last, preferred_element_type=jnp.float32
        )
        drafts = jnp.where(causal, drafts, masked_score)
        row_max = jnp.maximum(
            jnp.max(cached, axis=1, keepdims=True), jnp.max(drafts, axis=1, keepdims=True)
        )
        cached = jnp.exp2((cached - row_max) * log_scale)
        drafts = jnp.exp2((drafts - row_max) * log_scale)
        denominator = jnp.sum(cached, axis=1, keepdims=True) + jnp.sum(drafts, axis=1, keepdims=True)
        attended = jnp.dot(cached.astype(jnp.bfloat16), values, preferred_element_type=jnp.float32)
        attended = attended + jnp.dot(
            drafts.astype(jnp.bfloat16), draft_ref[n, window:, :], preferred_element_type=jnp.float32
        )
        attended = (attended / denominator).astype(jnp.bfloat16)
        for h in range(rows // window):
            out_ref[n * window : (n + 1) * window, h * head_dim : (h + 1) * head_dim] = attended[
                h * window : (h + 1) * window
            ]


def attend(table, visible, offsets, queries, drafts, sources, plan, window, per_step=2):
    requests, rows, head_dim = queries.shape
    slots = sum(length for _, _, length in plan)
    return pl.pallas_call(
        functools.partial(attend_kernel, per_step, plan),
        out_shape=jax.ShapeDtypeStruct((requests * window, rows // window * head_dim), jnp.bfloat16),
        grid_spec=pltpu.PrefetchScalarGridSpec(
            num_scalar_prefetch=3,
            grid=(requests // per_step,),
            in_specs=[
                pl.BlockSpec((per_step, rows, head_dim), lambda i, *_: (i, 0, 0)),
                pl.BlockSpec((per_step,) + drafts.shape[1:], lambda i, *_: (i, 0, 0)),
            ]
            + [pl.BlockSpec(memory_space=pl.ANY)] * len(sources),
            out_specs=pl.BlockSpec(
                (per_step * window, rows // window * head_dim), lambda i, *_: (i, 0)
            ),
            scratch_shapes=[
                pltpu.VMEM((slots + 1,) + sources[0].shape[1:], sources[0].dtype),
                pltpu.SemaphoreType.DMA((len(plan),)),
            ],
        ),
        cost_estimate=pl.CostEstimate(flops=1 << 30, bytes_accessed=10 << 20, transcendentals=1 << 21),
        name="attend",
    )(table, visible, offsets, queries, drafts, *sources)


def ring_starts(counts):
    middle = counts[..., 4]
    up = jnp.stack([over(middle + 1, 2), counts[..., 3], counts[..., 2]], axis=-2)
    down = jnp.stack([over(middle, 2), counts[..., 5], counts[..., 6]], axis=-2)
    both = jnp.stack([up, down], axis=-3)
    flat = both.reshape(both.shape[:-2] + (12,))
    before = (jnp.arange(12)[:, None] < jnp.arange(12)[None, :]).astype(jnp.int32)
    starts = jnp.sum(flat[..., :, None] * before, axis=-2).reshape(both.shape)
    group = both.sum(axis=-1)
    upto = (jnp.arange(3)[:, None] <= jnp.arange(3)[None, :]).astype(jnp.int32)
    travelling = jnp.sum(group[..., :, None] * upto, axis=-2)
    return starts, travelling


def by_distance(near, up, down, axis):
    part = lambda array, g: lax.slice_in_dim(array, g, g + 1, axis=axis)
    tables = []
    for middle in (up, down):
        parts = [near[0], near[1], part(up, 2), part(up, 1), part(middle, 0), part(down, 1), part(down, 2), near[2]]
        tables.append(jnp.concatenate(parts, axis=axis))
    return tables


def neighbours(ring_len, y_len):
    size = y_len * ring_len
    return (
        [(i, i // ring_len * ring_len + (i + 1) % ring_len) for i in range(size)],
        [(i, i // ring_len * ring_len + (i - 1) % ring_len) for i in range(size)],
        [(i, (i + ring_len) % size) for i in range(size)],
        [(i, (i - ring_len) % size) for i in range(size)],
    )


def first_moves(outputs, along, full):
    own, for_forth, for_back, rising, falling = outputs
    up, down, forth, back = along
    for _ in range(1, 3):
        rising = lax.ppermute(rising, "dp", up)
        falling = lax.ppermute(falling, "dp", down)
    forth_0 = lax.ppermute(for_forth, "dp", forth)
    back_0 = lax.ppermute(for_back, "dp", back)
    forth_00 = lax.ppermute(lax.slice_in_dim(forth_0, 3 * full, 5 * full), "dp", forth)
    back_00 = lax.ppermute(lax.slice_in_dim(back_0, 3 * full, 4 * full), "dp", back)
    return own, forth_0, back_0, forth_00, back_00, rising, falling


def along_rings(carried, offsets, along, capacity, room):
    own, forth_0, back_0, forth_00, back_00, rising, falling = carried
    up, down, forth, back = along
    full, half = capacity, capacity // 2
    arrays = [own, forth_0, back_0, forth_00, back_00]
    home = [(0, ("at", 0), full), (1, ("at", 0), full), (3, ("at", 0), full), (2, ("at", 0), full)]
    for_up = [(0, ("at", full), full), (1, ("at", full), full), (3, ("at", full), full), (2, ("at", full), full)]
    for_down = [(0, ("at", 2 * full), full), (1, ("at", 2 * full), full), (4, ("at", 0), full), (2, ("at", 2 * full), full)]
    found = {}

    def keep(array):
        arrays.append(array)
        return len(arrays) - 1

    passing_forth = passing_back = None
    for t in range(2, 5):
        u, d = keep(rising), keep(falling)
        if t < 4:
            rising = lax.ppermute(lax.slice_in_dim(rising, 0, room[t]), "dp", up)
            falling = lax.ppermute(lax.slice_in_dim(falling, 0, room[t]), "dp", down)
        length = full if t < 4 else half

        def piece(direction, r):
            number = ((t - 2) * 2 + direction) * 4 + r
            return ((u, d)[direction], ("offset", number), length)

        found[0, t, 0], found[1, t, 0] = piece(0, 0), piece(1, 0)
        forward = [piece(0, 1), piece(1, 1), piece(0, 2)]
        backward = [piece(0, 3), piece(1, 3), piece(1, 2)]
        for plan, passing in ((forward, passing_forth), (backward, passing_back)):
            if passing is not None:
                plan.append((passing[0], ("at", passing[1]), passing[2]))
        needed = sorted({p[0] for p in forward + backward})
        renamed = [
            [(needed.index(source), start, n) for source, start, n in plan]
            for plan in (forward, backward)
        ]
        send_forth, send_back = pick(offsets, [arrays[i] for i in needed], renamed)
        f = keep(lax.ppermute(send_forth, "dp", forth))
        b = keep(lax.ppermute(send_back, "dp", back))
        found[0, t, 1], found[1, t, 1] = (f, ("at", 0), length), (f, ("at", length), length)
        found[0, t, 3], found[1, t, 3] = (b, ("at", 0), length), (b, ("at", length), length)
        if t > 2:
            found[0, t - 1, 2] = (f, ("at", 3 * length), full)
            found[1, t - 1, 2] = (b, ("at", 3 * length), full)
        passing_forth, passing_back = (f, 2 * length, length), (b, 2 * length, length)
    near_up, near_down = pick(offsets, arrays[:5], [for_up, for_down])
    near_up = keep(lax.ppermute(near_up, "dp", up))
    near_down = keep(lax.ppermute(near_down, "dp", down))
    last_forth = lax.slice_in_dim(arrays[passing_forth[0]], 2 * half, 3 * half)
    last_back = lax.slice_in_dim(arrays[passing_back[0]], 2 * half, 3 * half)
    found[0, 4, 2] = (keep(lax.ppermute(last_forth, "dp", forth)), ("at", 0), half)
    found[1, 4, 2] = (keep(lax.ppermute(last_back, "dp", back)), ("at", 0), half)
    plan = home + [(near_up, ("at", 0), 4 * full), (near_down, ("at", 0), 4 * full)]
    plan += [found[direction, t, r] for t in range(2, 5) for direction in range(2) for r in range(4)]
    return arrays, plan


def project(token_rows, out_weight, column_count):
    size = lax.axis_size("mp")
    chips = size // 2
    place = lax.axis_index("mp")
    core = rest(place, 2)
    swap = [(i, i ^ 1) for i in range(size)]
    right = [(i, (i + 2) % size) for i in range(size)]
    left = [(i, (i - 2) % size) for i in range(size)]

    def columns(k, c):
        chip = rest(over(place, 2) + k, chips)
        return lax.dynamic_slice_in_dim(out_weight, (chip * 2 + c) * column_count, column_count, 1)

    own_weight = [columns(k, core) for k in range(chips)]
    given = jnp.concatenate([columns(k, 1 - core) for k in range(chips)], axis=0)
    their_weight = jnp.split(lax.ppermute(given, "mp", swap), chips, axis=0)
    theirs = lax.ppermute(token_rows, "mp", swap)

    def own_part(k):
        own = jnp.dot(token_rows, own_weight[k], preferred_element_type=jnp.float32)
        return lax.optimization_barrier(own)

    own_far = own_part(2)
    own_ahead = own_part(1)

    def with_theirs(own, k):
        return own + jnp.dot(theirs, their_weight[k], preferred_element_type=jnp.float32)

    half = column_count // 2
    far = with_theirs(own_far, 2).astype(jnp.bfloat16)
    from_left = lax.ppermute(far[:, :half], "mp", right)
    from_right = lax.ppermute(far[:, half:], "mp", left)
    ahead = with_theirs(own_ahead, 1)
    behind = with_theirs(own_part(3), 3)
    home = with_theirs(own_part(0), 0)
    ahead = jnp.concatenate([ahead[:, :half] + from_left.astype(jnp.float32), ahead[:, half:]], axis=1)
    behind = jnp.concatenate([behind[:, :half], behind[:, half:] + from_right.astype(jnp.float32)], axis=1)
    from_left = lax.ppermute(ahead.astype(jnp.bfloat16), "mp", right)
    from_right = lax.ppermute(behind.astype(jnp.bfloat16), "mp", left)
    return home + from_left.astype(jnp.float32) + from_right.astype(jnp.float32)


def on_device(
    queries,
    draft_kv,
    kv_pool,
    block_dest,
    block_table,
    context_len,
    draft_len,
    accept_mask,
    out_weight,
    residual,
    norm_gain,
):
    rank_count = lax.axis_size("dp")
    pool_count = kv_pool.shape[0]
    capacity = 2 * pool_count // rank_count
    requests, heads_local, window, head_dim = queries.shape
    block_len = kv_pool.shape[3]
    pool = kv_pool.reshape(pool_count, 2 * block_len, head_dim)
    queries = queries.reshape(requests, heads_local * window, head_dim)
    drafts = draft_kv.reshape(requests, 2 * window, head_dim)
    kept_count = jnp.sum(jnp.cumprod(accept_mask, axis=1, dtype=jnp.int32), axis=1, dtype=jnp.int32)
    visible = context_len - window + kept_count

    rank = lax.axis_index("dp")
    rank_y, rank_z = over(rank, ring_len), rest(rank, ring_len)
    y_len = rank_count // ring_len
    ahead_y = rest(over(block_dest, ring_len) - rank_y, y_len)
    ahead_z = rest(block_dest - rank_z, ring_len)
    ahead = jnp.where(block_dest >= 0, ahead_y * ring_len + ahead_z, rank_count)
    steps = jnp.arange(rank_count, dtype=jnp.int32)
    counts = jnp.sum((ahead[None, :] == steps[:, None]).astype(jnp.int32), axis=1, dtype=jnp.int32)
    starts, _ = ring_starts(counts.reshape(y_len, ring_len))
    fixed = jnp.array([[0, 3, 6, 8], [1, 4, 7, 9], [2, 5, 11, 10]], jnp.int32) * capacity
    near_slots = 12 * capacity
    tables = by_distance(
        [fixed[n : n + 1] for n in range(3)],
        near_slots + starts[0],
        near_slots + room[0] + starts[1],
        0,
    )
    start = jnp.stack([table.T for table in tables], axis=-1).reshape(-1)
    outputs = pack_blocks(
        ahead,
        jnp.concatenate([start, jnp.zeros((2,), jnp.int32)]),
        pool,
        (3 * capacity, 5 * capacity, 4 * capacity, room[0], room[0]),
        lambda d: (d & (ring_len - 1)) == ring_len // 2,
    )
    along = neighbours(ring_len, y_len)
    carried = first_moves(outputs, along, capacity)

    all_counts = from_everyone(counts, "dp").reshape(rank_count, y_len, ring_len)
    all_starts, travelling = ring_starts(all_counts)
    limits = jnp.array(room[:0:-1], jnp.int32)
    fits = jnp.all(travelling <= limits)
    lengths = jnp.array([capacity // 2, capacity, capacity], jnp.int32)
    clamped = jnp.minimum(all_starts, (limits - lengths)[:, None])
    first = jnp.arange(24, dtype=jnp.int32).reshape(3, 2, 4)
    base = jnp.where(first >= 16, 28 * capacity + (first - 16) * (capacity // 2), (12 + first) * capacity)
    base = base[::-1].transpose(1, 0, 2) + all_starts - clamped
    by_r = jnp.arange(y_len, dtype=jnp.int32) * capacity
    near = [
        jnp.broadcast_to(n * y_len * capacity + by_r, (rank_count, 1, y_len)) for n in range(3)
    ]
    even, odd = by_distance(near, base[:, 0], base[:, 1], 1)
    source = jnp.arange(rank_count, dtype=jnp.int32)
    gap_y = rest(rank_y - over(source, ring_len), y_len)
    gap_z = rest(rank_z - source, ring_len)
    here = (gap_z[:, None, None] == jnp.arange(ring_len)[None, :, None]) & (
        gap_y[:, None, None] == jnp.arange(y_len)[None, None, :]
    )
    even = jnp.sum(jnp.where(here, even, 0), axis=(1, 2))
    odd = jnp.sum(jnp.where(here, odd, 0), axis=(1, 2))
    halved = gap_z == ring_len // 2
    steps_z = jnp.arange(2, 5, dtype=jnp.int32)[:, None] * jnp.array([1, -1], jnp.int32)[None]
    origin = rank_y * ring_len + rest(rank_z - steps_z, ring_len)
    chosen = (origin[:, :, None] == source[None, None, :]).astype(jnp.int32)
    by_step = clamped[:, :, ::-1].transpose(2, 1, 0, 3)
    offsets = jnp.sum(by_step * chosen[..., None], axis=2).reshape(-1)
    origin = over(block_table, capacity)
    order = rest(block_table, capacity)
    named = origin[:, :, None] == source[None, None, :]
    pick_from = lambda values: jnp.sum(jnp.where(named, values, 0), axis=2)
    table = jnp.where(rest(order, 2) == 0, pick_from(even), pick_from(odd))
    table = table + jnp.where(pick_from(halved.astype(jnp.int32)) > 0, over(order, 2), order)
    table, offsets, visible, fits = lax.optimization_barrier((table.reshape(-1), offsets, visible, fits))

    def by_rings(*carried):
        arrays, plan = along_rings(carried, offsets, along, capacity, room)
        return attend(table, visible, offsets, queries, drafts, arrays, plan, window)

    def by_exchange(*carried):
        start = jnp.repeat(jnp.arange(rank_count + 1, dtype=jnp.int32) * capacity, 2)
        dest = jnp.where(block_dest >= 0, block_dest, rank_count)
        slots = rank_count * capacity
        (packed,) = pack_blocks(dest, start, pool, (slots,), lambda d: d < 0)
        arrived = lax.all_to_all(packed, "dp", split_axis=0, concat_axis=0, tiled=True)
        piece = slots // load_pieces
        plan = [(0, ("at", p * piece), piece) for p in range(load_pieces)]
        no_offsets = jnp.zeros((1,), jnp.int32)
        return attend(block_table.reshape(-1), visible, no_offsets, queries, drafts, [arrived], plan, window, 1)

    token_rows = lax.cond(fits, by_rings, by_exchange, *carried)
    column_count = norm_gain.shape[0]
    place = lax.axis_index("mp")
    live_rows = (jnp.arange(window, dtype=jnp.int32)[None, :] < draft_len[:, None]).reshape(
        requests * window
    )
    share = project(token_rows, out_weight, column_count)
    local_residual = lax.dynamic_slice_in_dim(residual, place * column_count, column_count, 1)
    local_hidden = local_residual.astype(jnp.float32) + share
    squares = over_copies(jnp.sum(local_hidden * local_hidden, axis=1), "mp")
    mean_square = (squares / (column_count * lax.axis_size("mp")))[:, None]
    normed = local_hidden * lax.rsqrt(mean_square + norm_epsilon) * norm_gain[None, :]
    return jnp.where(live_rows[:, None], normed, 0.0).astype(jnp.bfloat16)


def solution(mesh):
    return jax.shard_map(
        on_device,
        mesh=mesh,
        in_specs=(
            P("dp", "mp", None, None),
            P("dp", None, "mp", None, None),
            P("dp", None, "mp", None, None),
            P("dp"),
            P("dp", None),
            P("dp"),
            P("dp"),
            P("dp", None),
            P("mp", None),
            P("dp", None),
            P("mp"),
        ),
        out_specs=P("dp", "mp"),
        check_vma=False,
    )
```

time: 284 us -> 244 us (0.86)
  waiting for transfers between devices: 200 us -> 77.7 us
  starting transfers between devices: 26.2 us -> 61.1 us
  local copies, waits for them, and re-layouts: 6.36 us -> 24.9 us
  other arithmetic: 3.56 us -> 21.1 us
  Pallas kernels: 25.7 us -> 39.1 us
    all_to_all x1 -> x0, waiting for transfers between devices: 181 us -> none  [on_device(): lax.all_to_all(outgoing, 'dp', split_axis=0, concat_axis=0, tiled=True)]
    ppermute x0 -> x22, waiting for transfers between devices: none -> 57.9 us  [the longest x3 31.6 us: along_rings(): f = keep(lax.ppermute(send_forth, 'dp', forth))]
    ppermute x0 -> x22, starting transfers between devices: none -> 29.9 us  [the longest x3 5.13 us: along_rings(): b = keep(lax.ppermute(send_back, 'dp', back))]
    pallas_call x2 -> x6, Pallas kernels: 25.7 us -> 39.1 us  [the longest x1 18.9 us: attend(): pl.pallas_call(functools.partial(attend_kernel, per_step, plan), out_shap...]
    all_to_all x1 -> x2, starting transfers between devices: 5.27 us -> 17.6 us  [from_everyone(): lax.all_to_all(jnp.broadcast_to(array[None], (length, *array.shape)), axi...]
    all_to_all x1 -> x0, starting transfers between devices: 12 us -> none  [on_device(): lax.all_to_all(outgoing, 'dp', split_axis=0, concat_axis=0, tiled=True)]
    slice x0 -> x12, local copies, waits for them, and re-layouts: none -> 9.58 us  [the longest x2 2.95 us: along_rings(): falling = lax.ppermute(lax.slice_in_dim(falling, 0, room[t]), 'dp', down)]
    reduce_sum x0 -> x9, other arithmetic: none -> 8.25 us  [the longest x1 2.58 us: on_device(): pick_from = lambda values: jnp.sum(jnp.where(named, values, 0), axis=2)]
  transfers between devices with their start and end apart: 8 -> 30, of which waited for: 6 -> 15; matrix products, arithmetic and copies ran while one was open for 8% -> 22% of each run, Pallas kernels for 7% -> 7%
where the time goes in v3:
time: 244 us; the launch traced here: 242 us
  waiting for transfers between devices  77.7 us (32%)
  starting transfers between devices  61.1 us (25%)
  Pallas kernels  39.1 us (16%)
  local copies, waits for them, and re-layouts  24.9 us (10%)
  other arithmetic  21.1 us (9%)
  matrix products  16.7 us (7%)
    ppermute x3, waiting for transfers between devices, along_rings(): f = keep(lax.ppermute(send_forth, 'dp', forth))  31.6 us
    ppermute x2, waiting for transfers between devices, first_moves(): rising = lax.ppermute(rising, 'dp', up)  22.8 us
    pallas_call x1, Pallas kernels, attend(): pl.pallas_call(functools.partial(attend_kernel, per_step, plan), out_shap...  18.9 us
    all_to_all x2, starting transfers between devices, from_everyone(): lax.all_to_all(jnp.broadcast_to(array[None], (length, *array.shape)), axi...  17.6 us
    pallas_call x4, Pallas kernels, pick(): pl.pallas_call(functools.partial(pick_kernel, plans), out_shape=[jax.Shap...  11.9 us
    dot_general x4, matrix products, own_part(): own = jnp.dot(token_rows, own_weight[k], preferred_element_type=jnp.float32)  9 us
    pallas_call x1, Pallas kernels, pack_blocks(): pl.pallas_call(functools.partial(pack_kernel, halved, kinds), out_shape=[...  8.26 us
    dot_general x4, matrix products, with_theirs(): jnp.dot(theirs, their_weight[k], preferred_element_type=jnp.float32)  7.72 us
  transfers between devices with their start and end apart: 30, of which 15 were waited for; matrix products, arithmetic and copies ran while one was open for 22% of the time, Pallas kernels for 7%

profile of v3, /device:TPU:1, one launch (start us, length us, event | category | flops | bytes accessed | tf_op | source)
XLA Modules:
  0.0 241.9 jit_solution(2800005383550135123)
XLA Ops:
  1.5 12.0 %all-to-all-start.1 = ((s32[32,1,32]{2,1,0:T(1,128)}), s32[32,1,32]{2,1,0:T(1,128)S(1)}, u32[]{:S(2)}, u32[]{:S(2)}) async-start(s32[32,1,32]{2,1,0:T(1,128)} %broadcast_in_dim.103), calls=%async_computation.1 | async-start | bytes 32768 | tf_op jit(solution)/shard_map/all_to_all | solution.py:29
  17.0 8.3 %pack_blocks.3 = (bf16[96,32,128]{2,1,0:T(8,128)(2,1)S(1)}, bf16[160,32,128]{2,1,0:T(8,128)(2,1)}, bf16[128,32,128]{2,1,0:T(8,128)(2,1)}, bf16[168,32,128]{2,1,0:T(8,128)(2,1)}, bf16[168,32,128]{2,1,0:T(8,128)(2,1)}) custom-call(s32[512]{0:T(512)} %copy-done.6, s32[66]{0:T(128)} %concatenate.36.start_ref, bf16[512,32,128]{2,1,0:T(8,128)(2,1)} %bitcast.50), custom_call_target="tpu_custom_call" | custom-call | flops 268435456 | bytes 8388608 | tf_op jit(solution)/shard_map/pack_blocks/pallas_call | solution.py:74
  35.4 2.5 %constant_dynamic-slice_fusion.3 = (bf16[1024,512]{1,0:T(8,128)(2,1)S(1)}, bf16[1024,512]{1,0:T(8,128)(2,1)S(1)}, bf16[1024,512]{1,0:T(8,128)(2,1)S(1)}, bf16[1024,512]{1,0:T(8,128)(2,1)S(1)}) fusion(bf16[1024,4096]{1,0:T(8,128)(2,1)} %param.25, s32[]{:T(128)S(6)} %select_n.77, s32[]{:T(128)S(6)} %select_n.80, s32[]{:T(128)S(6)} %select_n.79, s32[]{:T(128)S(6)} %select_n.78), kind=kLoop, calls=%fused_computation.86 | loop fusion | bytes 8388624 | tf_op jit(solution)/shard_map/dynamic_slice | solution.py:338
  42.3 15.3 %collective-permute-done.14 = bf16[168,32,128]{2,1,0:T(8,128)(2,1)} collective-permute-done((bf16[168,32,128]{2,1,0:T(8,128)(2,1)}, bf16[168,32,128]{2,1,0:T(8,128)(2,1)}, u32[]{:S(2)}, u32[]{:S(2)}) %collective-permute-start.14) | collective-permute-done | bytes 1376288 | tf_op jit(solution)/shard_map/ppermute | solution.py:260
  57.6 2.7 %collective-permute-start.17 = (bf16[168,32,128]{2,1,0:T(8,128)(2,1)}, bf16[168,32,128]{2,1,0:T(8,128)(2,1)S(1)}, u32[]{:S(2)}, u32[]{:S(2)}) collective-permute-start(bf16[168,32,128]{2,1,0:T(8,128)(2,1)} %collective-permute-done.16), channel_id=1, source_target_pairs={{0,56},{8,0},{16,8},{24,16},{32,24},{40,32},{48,40},{56,48},{64,12... | collective-permute-start | bytes 4128776 | tf_op jit(solution)/shard_map/ppermute | solution.py:261
  63.0 2.6 %select_reduce_fusion = (s32[32,32]{1,0:T(8,128)S(1)}, s32[32,32]{1,0:T(8,128)S(1)}, s32[32,32]{1,0:T(8,128)S(1)}) fusion(s32[32]{0:T(128)} %compare_convert_fusion.1, s32[32,32]{1,0:T(8,128)} %broadcast_shift-right-arithmetic_fusion, s32[32]{0:T(128)S(1)} %get-tuple-element.97, s32[32]{0:T(128)S(1)} %get-tuple-element.98), kind=kLoop, calls=%fused_computation.31 | loop fusion | flops 226304 | bytes 16768 | tf_op jit(solution)/shard_map/reduce_sum | solution.py:452
  81.4 7.5 %collective-permute-done.15 = bf16[168,32,128]{2,1,0:T(8,128)(2,1)S(1)} collective-permute-done((bf16[168,32,128]{2,1,0:T(8,128)(2,1)}, bf16[168,32,128]{2,1,0:T(8,128)(2,1)S(1)}, u32[]{:S(2)}, u32[]{:S(2)}) %collective-permute-start.15) | collective-permute-done | bytes 1376288 | tf_op jit(solution)/shard_map/ppermute | solution.py:260
  89.0 92.7 %conditional.1 = (bf16[512,1024]{1,0:T(8,128)(2,1)}) conditional(s32[]{:T(128)} %convert_element_type.66, (s32[32,32]{1,0:T(8,128)S(1)}, s32[512]{0:T(512)}, bf16[512,32,128]{2,1,0:T(8,128)(2,1)}, s32[32]{0:T(128)}, bf16[32,128,128]{2,1,0:T(8,128)(2,1)}, /*index=5*/bf16[32,32,128]{2,1,0:T(8,128)(2,1)}) %tuple.52, (s32[24]{0:T(128)}, ...), branch_computations={%region_14.15_spmd, %region_15.16_spmd} | conditional | flops 1342178304 | bytes 79709768 | solution.py:472
  91.5 2.3 collective-permute-start.3
  98.6 14.7 %collective-permute-done.refs_0_.refs_7_ = bf16[96,32,128]{2,1,0:T(8,128)(2,1)} collective-permute-done((bf16[96,32,128]{2,1,0:T(8,128)(2,1)}, bf16[96,32,128]{2,1,0:T(8,128)(2,1)}, u32[]{:S(2)}, u32[]{:S(2)}) %collective-permute-start) | collective-permute-done | bytes 786464 | tf_op jit(solution)/shard_map/cond/branch_1_fun/ppermute | solution.py:307
  113.8 3.5 %pick.5 = (bf16[128,32,128]{2,1,0:T(8,128)(2,1)}, bf16[128,32,128]{2,1,0:T(8,128)(2,1)}) custom-call(s32[24]{0:T(128)S(1)} %copy-done.7, bf16[96,32,128]{2,1,0:T(8,128)(2,1)} %collective-permute-done.refs_0_.refs_7_, bf16[96,32,128]{2,1,0:T(8,128)(2,1)} %collective-permute-done.1.refs_1_.refs_8_, ...), custom_call_target="tpu_custom_call" | custom-call | flops 1048576 | bytes 4194304 | tf_op jit(solution)/shard_map/cond/branch_1_fun/pick/pallas_call | solution.py:118
  126.4 3.3 %pick.7 = (bf16[128,32,128]{2,1,0:T(8,128)(2,1)}, bf16[128,32,128]{2,1,0:T(8,128)(2,1)}) custom-call(s32[24]{0:T(128)S(1)} %copy-done.7, bf16[96,32,128]{2,1,0:T(8,128)(2,1)S(1)} %get-tuple-element.55.refs_0_, bf16[160,32,128]{2,1,0:T(8,128)(2,1)} %get-tuple-element.56.refs_1_, bf16[128,32,128]{2,1,0:T(8,128)(2,1)} %get-tuple-element.57.refs_2_, ...), custom_call_target="tpu_custom_call" | custom-call | flops 1048576 | bytes 4194304 | tf_op jit(solution)/shard_map/cond/branch_1_fun/pick/pallas_call | solution.py:118
  133.3 6.5 %collective-permute-done.4.refs_0_.refs_11_ = bf16[128,32,128]{2,1,0:T(8,128)(2,1)} collective-permute-done((bf16[128,32,128]{2,1,0:T(8,128)(2,1)}, bf16[128,32,128]{2,1,0:T(8,128)(2,1)}, u32[]{:S(2)}, u32[]{:S(2)}) %collective-permute-start.4) | collective-permute-done | bytes 1048608 | tf_op jit(solution)/shard_map/cond/branch_1_fun/ppermute | solution.py:307
  139.8 3.0 %pick.6 = (bf16[80,32,128]{2,1,0:T(8,128)(2,1)}, bf16[80,32,128]{2,1,0:T(8,128)(2,1)}) custom-call(s32[24]{0:T(128)S(1)} %copy-done.7, bf16[128,32,128]{2,1,0:T(8,128)(2,1)} %collective-permute-done.4.refs_0_.refs_11_, bf16[128,32,128]{2,1,0:T(8,128)(2,1)} %collective-permute-done.5.refs_1_.refs_12_, ...), custom_call_target="tpu_custom_call" | custom-call | flops 1048576 | bytes 4194304 | tf_op jit(solution)/shard_map/cond/branch_1_fun/pick/pallas_call | solution.py:118
  145.6 10.4 %collective-permute-done.8.refs_15_ = bf16[80,32,128]{2,1,0:T(8,128)(2,1)S(1)} collective-permute-done((bf16[80,32,128]{2,1,0:T(8,128)(2,1)}, bf16[80,32,128]{2,1,0:T(8,128)(2,1)S(1)}, u32[]{:S(2)}, u32[]{:S(2)}) %collective-permute-start.8) | collective-permute-done | bytes 655392 | tf_op jit(solution)/shard_map/cond/branch_1_fun/ppermute | solution.py:307
  157.9 2.7 %collective-permute-start.13 = (bf16[16,32,128]{2,1,0:T(8,128)(2,1)S(1)}, bf16[16,32,128]{2,1,0:T(8,128)(2,1)}, u32[]{:S(2)}, u32[]{:S(2)}) collective-permute-start(bf16[16,32,128]{2,1,0:T(8,128)(2,1)S(1)} %slice.179), channel_id=1, source_target_pairs={{0,192},{8,200},{16,208},{24,216},{32,224},{40,232},{48,240},{56,2... | collective-permute-start | bytes 393224 | tf_op jit(solution)/shard_map/cond/branch_1_fun/ppermute | solution.py:321
  162.6 18.9 %attend.3 = bf16[512,1024]{1,0:T(8,128)(2,1)} custom-call(s32[1024]{0:T(1024)S(1)} %copy-done.8, s32[32]{0:T(128)S(1)} %copy-done.12, s32[24]{0:T(128)S(1)} %copy-done.7, bf16[32,128,128]{2,1,0:T(8,128)(2,1)} %get-tuple-element.53.queries_ref, bf16[32,32,128]{2,1,0:T(8,128)(2,1)} %get-tuple-element.54.draft_ref, ...), custom_call_target="tpu_custom_call" | custom-call | flops 1073741824 | bytes 10485760 | tf_op jit(solution)/shard_map/cond/branch_1_fun/attend/pallas_call | solution.py:199
  181.7 7.2 %collective-permute-start.23 = (bf16[4096,512]{1,0:T(8,128)(2,1)}, bf16[4096,512]{1,0:T(8,128)(2,1)}, u32[]{:S(2)}, u32[]{:S(2)}) collective-permute-start(bf16[4096,512]{1,0:T(8,128)(2,1)} %pad_maximum_fusion), channel_id=1, source_target_pairs={{0,1},{1,0},{2,3},{3,2},{4,5},{5,4},{6,7},{7,6},{8,9},{9,8},{10,11... | collective-permute-start | bytes 12582920 | tf_op jit(solution)/shard_map/ppermute | solution.py:342
  199.7 2.6 %collective-permute-start.26 = (bf16[512,256]{1,0:T(8,128)(2,1)S(1)}, bf16[512,256]{1,0:T(8,128)(2,1)S(1)}, u32[]{:S(2)}, u32[]{:S(2)}) collective-permute-start(bf16[512,256]{1,0:T(8,128)(2,1)S(1)} %get-tuple-element.106), channel_id=1, source_target_pairs={{0,6},{1,7},{2,0},{3,1},{4,2},{5,3},{6,4},{7,5},{8,14},{9,15},{10,... | collective-permute-start | bytes 786440 | tf_op jit(solution)/shard_map/ppermute | solution.py:358
  207.7 3.5 %collective-permute-start.27 = (bf16[512,512]{1,0:T(8,128)(2,1)S(1)}, bf16[512,512]{1,0:T(8,128)(2,1)S(1)}, u32[]{:S(2)}, u32[]{:S(2)}) collective-permute-start(bf16[512,512]{1,0:T(8,128)(2,1)S(1)} %pad_maximum_fusion.2), channel_id=1, source_target_pairs={{0,6},{1,7},{2,0},{3,1},{4,2},{5,3},{6,4},{7,5},{8,14},{9,15},{10,... | collective-permute-start | bytes 1572872 | tf_op jit(solution)/shard_map/ppermute | solution.py:365
  211.1 4.0 %collective-permute-done.24 = bf16[512,256]{1,0:T(8,128)(2,1)S(1)} collective-permute-done((bf16[512,256]{1,0:T(8,128)(2,1)S(1)}, bf16[512,256]{1,0:T(8,128)(2,1)S(1)}, u32[]{:S(2)}, u32[]{:S(2)}) %collective-permute-start.24) | collective-permute-done | bytes 262176 | tf_op jit(solution)/shard_map/ppermute | solution.py:357
  221.2 7.3 %collective-permute-done.25 = bf16[512,512]{1,0:T(8,128)(2,1)S(1)} collective-permute-done((bf16[512,512]{1,0:T(8,128)(2,1)S(1)}, bf16[512,512]{1,0:T(8,128)(2,1)S(1)}, u32[]{:S(2)}, u32[]{:S(2)}) %collective-permute-start.25) | collective-permute-done | bytes 524320 | tf_op jit(solution)/shard_map/ppermute | solution.py:364
  230.6 5.6 %all-to-all-start.2 = ((f32[8,1,512]{2,1,0:T(1,128)}), f32[8,1,512]{2,1,0:T(1,128)S(1)}, u32[]{:S(2)}, u32[]{:S(2)}) async-start(f32[8,1,512]{2,1,0:T(1,128)} %broadcast_in_dim.110), calls=%async_computation.2 | async-start | bytes 32768 | tf_op jit(solution)/shard_map/all_to_all | solution.py:29
  236.3 4.5 %all-to-all-done.2 = f32[8,1,512]{2,1,0:T(1,128)S(1)} async-done(((f32[8,1,512]{2,1,0:T(1,128)}), f32[8,1,512]{2,1,0:T(1,128)S(1)}, u32[]{:S(2)}, u32[]{:S(2)}) %all-to-all-start.2) | async-done | bytes 16416 | tf_op jit(solution)/shard_map/all_to_all | solution.py:29
  (180 shorter events, 89.7 us)
Async XLA Ops:
  1.5 39.1 %all-to-all-start.1 = ((s32[32,1,32]{2,1,0:T(1,128)}), s32[32,1,32]{2,1,0:T(1,128)S(1)}, u32[]{:S(2)}, u32[]{:S(2)}) async-start(s32[32,1,32]{2,1,0:T(1,128)} %broadcast_in_dim.103), calls=%async_computation.1 | async-start | bytes 32768 | tf_op jit(solution)/shard_map/all_to_all | solution.py:29
  25.2 32.4 %collective-permute-start.14 = (bf16[168,32,128]{2,1,0:T(8,128)(2,1)}, bf16[168,32,128]{2,1,0:T(8,128)(2,1)}, u32[]{:S(2)}, u32[]{:S(2)}) collective-permute-start(bf16[168,32,128]{2,1,0:T(8,128)(2,1)} %get-tuple-element.82), channel_id=1, source_target_pairs={{0,8},{8,16},{16,24},{24,32},{32,40},{40,48},{48,56},{56,0},{64,72... | collective-permute-start | bytes 4128776 | tf_op jit(solution)/shard_map/ppermute | solution.py:260
  26.5 31.1 %collective-permute-start.16 = (bf16[168,32,128]{2,1,0:T(8,128)(2,1)}, bf16[168,32,128]{2,1,0:T(8,128)(2,1)}, u32[]{:S(2)}, u32[]{:S(2)}) collective-permute-start(bf16[168,32,128]{2,1,0:T(8,128)(2,1)} %get-tuple-element.83), channel_id=1, source_target_pairs={{0,56},{8,0},{16,8},{24,16},{32,24},{40,32},{48,40},{56,48},{64,12... | collective-permute-start | bytes 4128776 | tf_op jit(solution)/shard_map/ppermute | solution.py:261
  28.0 37.6 %collective-permute-start.18 = (bf16[160,32,128]{2,1,0:T(8,128)(2,1)}, bf16[160,32,128]{2,1,0:T(8,128)(2,1)}, u32[]{:S(2)}, u32[]{:S(2)}) collective-permute-start(bf16[160,32,128]{2,1,0:T(8,128)(2,1)} %get-tuple-element.85), channel_id=1, source_target_pairs={{0,64},{8,72},{16,80},{24,88},{32,96},{40,104},{48,112},{56,120},{... | collective-permute-start | bytes 3932168 | tf_op jit(solution)/shard_map/ppermute | solution.py:262
  29.2 39.8 %collective-permute-start.19 = (bf16[128,32,128]{2,1,0:T(8,128)(2,1)}, bf16[128,32,128]{2,1,0:T(8,128)(2,1)}, u32[]{:S(2)}, u32[]{:S(2)}) collective-permute-start(bf16[128,32,128]{2,1,0:T(8,128)(2,1)} %get-tuple-element.86), channel_id=1, source_target_pairs={{0,192},{8,200},{16,208},{24,216},{32,224},{40,232},{48,240},{56,2... | collective-permute-start | bytes 3145736 | tf_op jit(solution)/shard_map/ppermute | solution.py:263
  57.6 31.4 %collective-permute-start.15 = (bf16[168,32,128]{2,1,0:T(8,128)(2,1)}, bf16[168,32,128]{2,1,0:T(8,128)(2,1)S(1)}, u32[]{:S(2)}, u32[]{:S(2)}) collective-permute-start(bf16[168,32,128]{2,1,0:T(8,128)(2,1)} %collective-permute-done.14), channel_id=1, source_target_pairs={{0,8},{8,16},{16,24},{24,32},{32,40},{40,48},{48,56},{56,0},{64,72... | collective-permute-start | bytes 4128776 | tf_op jit(solution)/shard_map/ppermute | solution.py:260
  57.6 31.3 %collective-permute-start.17 = (bf16[168,32,128]{2,1,0:T(8,128)(2,1)}, bf16[168,32,128]{2,1,0:T(8,128)(2,1)S(1)}, u32[]{:S(2)}, u32[]{:S(2)}) collective-permute-start(bf16[168,32,128]{2,1,0:T(8,128)(2,1)} %collective-permute-done.16), channel_id=1, source_target_pairs={{0,56},{8,0},{16,8},{24,16},{32,24},{40,32},{48,40},{56,48},{64,12... | collective-permute-start | bytes 4128776 | tf_op jit(solution)/shard_map/ppermute | solution.py:261
  67.4 14.0 %collective-permute-start.20 = (bf16[64,32,128]{2,1,0:T(8,128)(2,1)}, bf16[64,32,128]{2,1,0:T(8,128)(2,1)}, u32[]{:S(2)}, u32[]{:S(2)}) collective-permute-start(bf16[64,32,128]{2,1,0:T(8,128)(2,1)} %slice.191), channel_id=1, source_target_pairs={{0,64},{8,72},{16,80},{24,88},{32,96},{40,104},{48,112},{56,120},{... | collective-permute-start | bytes 1572872 | tf_op jit(solution)/shard_map/ppermute | solution.py:264
  70.7 10.8 %collective-permute-start.21 = (bf16[32,32,128]{2,1,0:T(8,128)(2,1)}, bf16[32,32,128]{2,1,0:T(8,128)(2,1)}, u32[]{:S(2)}, u32[]{:S(2)}) collective-permute-start(bf16[32,32,128]{2,1,0:T(8,128)(2,1)} %slice.192), channel_id=1, source_target_pairs={{0,192},{8,200},{16,208},{24,216},{32,224},{40,232},{48,240},{56,2... | collective-permute-start | bytes 786440 | tf_op jit(solution)/shard_map/ppermute | solution.py:265
  90.0 23.3 %collective-permute-start.2 = (bf16[124,32,128]{2,1,0:T(8,128)(2,1)}, bf16[124,32,128]{2,1,0:T(8,128)(2,1)}, u32[]{:S(2)}, u32[]{:S(2)}) collective-permute-start(bf16[124,32,128]{2,1,0:T(8,128)(2,1)} %slice.104), channel_id=1, source_target_pairs={{0,8},{8,16},{16,24},{24,32},{32,40},{40,48},{48,56},{56,0},{64,72... | collective-permute-start | bytes 3047432 | tf_op jit(solution)/shard_map/cond/branch_1_fun/ppermute | solution.py:287
  91.5 22.3 %collective-permute-start.3 = (bf16[124,32,128]{2,1,0:T(8,128)(2,1)}, bf16[124,32,128]{2,1,0:T(8,128)(2,1)}, u32[]{:S(2)}, u32[]{:S(2)}) collective-permute-start(bf16[124,32,128]{2,1,0:T(8,128)(2,1)} %slice.105), channel_id=1, source_target_pairs={{0,56},{8,0},{16,8},{24,16},{32,24},{40,32},{48,40},{56,48},{64,12... | collective-permute-start | bytes 3047432 | tf_op jit(solution)/shard_map/cond/branch_1_fun/ppermute | solution.py:288
  95.8 17.5 %collective-permute-start = (bf16[96,32,128]{2,1,0:T(8,128)(2,1)}, bf16[96,32,128]{2,1,0:T(8,128)(2,1)}, u32[]{:S(2)}, u32[]{:S(2)}) collective-permute-start(bf16[96,32,128]{2,1,0:T(8,128)(2,1)} %get-tuple-element.62), channel_id=1, source_target_pairs={{0,64},{8,72},{16,80},{24,88},{32,96},{40,104},{48,112},{56,120},{... | collective-permute-start | bytes 2359304 | tf_op jit(solution)/shard_map/cond/branch_1_fun/ppermute | solution.py:307
  96.5 16.7 %collective-permute-start.1 = (bf16[96,32,128]{2,1,0:T(8,128)(2,1)}, bf16[96,32,128]{2,1,0:T(8,128)(2,1)}, u32[]{:S(2)}, u32[]{:S(2)}) collective-permute-start(bf16[96,32,128]{2,1,0:T(8,128)(2,1)} %get-tuple-element.63), channel_id=1, source_target_pairs={{0,192},{8,200},{16,208},{24,216},{32,224},{40,232},{48,240},{56,2... | collective-permute-start | bytes 2359304 | tf_op jit(solution)/shard_map/cond/branch_1_fun/ppermute | solution.py:308
  117.3 22.5 %collective-permute-start.4 = (bf16[128,32,128]{2,1,0:T(8,128)(2,1)}, bf16[128,32,128]{2,1,0:T(8,128)(2,1)}, u32[]{:S(2)}, u32[]{:S(2)}) collective-permute-start(bf16[128,32,128]{2,1,0:T(8,128)(2,1)} %get-tuple-element.64), channel_id=1, source_target_pairs={{0,64},{8,72},{16,80},{24,88},{32,96},{40,104},{48,112},{56,120},{... | collective-permute-start | bytes 3145736 | tf_op jit(solution)/shard_map/cond/branch_1_fun/ppermute | solution.py:307
  118.6 21.2 %collective-permute-start.5 = (bf16[128,32,128]{2,1,0:T(8,128)(2,1)}, bf16[128,32,128]{2,1,0:T(8,128)(2,1)}, u32[]{:S(2)}, u32[]{:S(2)}) collective-permute-start(bf16[128,32,128]{2,1,0:T(8,128)(2,1)} %get-tuple-element.65), channel_id=1, source_target_pairs={{0,192},{8,200},{16,208},{24,216},{32,224},{40,232},{48,240},{56,2... | collective-permute-start | bytes 3145736 | tf_op jit(solution)/shard_map/cond/branch_1_fun/ppermute | solution.py:308
  121.8 8.8 %collective-permute-start.6 = (bf16[52,32,128]{2,1,0:T(8,128)(2,1)}, bf16[52,32,128]{2,1,0:T(8,128)(2,1)}, u32[]{:S(2)}, u32[]{:S(2)}) collective-permute-start(bf16[52,32,128]{2,1,0:T(8,128)(2,1)} %slice.176), channel_id=1, source_target_pairs={{0,8},{8,16},{16,24},{24,32},{32,40},{40,48},{48,56},{56,0},{64,72... | collective-permute-start | bytes 1277960 | tf_op jit(solution)/shard_map/cond/branch_1_fun/ppermute | solution.py:287
  129.7 30.9 %collective-permute-start.10 = (bf16[128,32,128]{2,1,0:T(8,128)(2,1)}, bf16[128,32,128]{2,1,0:T(8,128)(2,1)}, u32[]{:S(2)}, u32[]{:S(2)}) collective-permute-start(bf16[128,32,128]{2,1,0:T(8,128)(2,1)} %get-tuple-element.68), channel_id=1, source_target_pairs={{0,8},{8,16},{16,24},{24,32},{32,40},{40,48},{48,56},{56,0},{64,72... | collective-permute-start | bytes 3145736 | tf_op jit(solution)/shard_map/cond/branch_1_fun/ppermute | solution.py:316
  130.6 30.0 %collective-permute-start.11 = (bf16[128,32,128]{2,1,0:T(8,128)(2,1)}, bf16[128,32,128]{2,1,0:T(8,128)(2,1)}, u32[]{:S(2)}, u32[]{:S(2)}) collective-permute-start(bf16[128,32,128]{2,1,0:T(8,128)(2,1)} %get-tuple-element.69), channel_id=1, source_target_pairs={{0,56},{8,0},{16,8},{24,16},{32,24},{40,32},{48,40},{56,48},{64,12... | collective-permute-start | bytes 3145736 | tf_op jit(solution)/shard_map/cond/branch_1_fun/ppermute | solution.py:317
  142.9 13.2 %collective-permute-start.8 = (bf16[80,32,128]{2,1,0:T(8,128)(2,1)}, bf16[80,32,128]{2,1,0:T(8,128)(2,1)S(1)}, u32[]{:S(2)}, u32[]{:S(2)}) collective-permute-start(bf16[80,32,128]{2,1,0:T(8,128)(2,1)} %get-tuple-element.66), channel_id=1, source_target_pairs={{0,64},{8,72},{16,80},{24,88},{32,96},{40,104},{48,112},{56,120},{... | collective-permute-start | bytes 1966088 | tf_op jit(solution)/shard_map/cond/branch_1_fun/ppermute | solution.py:307
  143.9 13.1 %collective-permute-start.9 = (bf16[80,32,128]{2,1,0:T(8,128)(2,1)}, bf16[80,32,128]{2,1,0:T(8,128)(2,1)S(1)}, u32[]{:S(2)}, u32[]{:S(2)}) collective-permute-start(bf16[80,32,128]{2,1,0:T(8,128)(2,1)} %get-tuple-element.67), channel_id=1, source_target_pairs={{0,192},{8,200},{16,208},{24,216},{32,224},{40,232},{48,240},{56,2... | collective-permute-start | bytes 1966088 | tf_op jit(solution)/shard_map/cond/branch_1_fun/ppermute | solution.py:308
  181.7 15.7 %collective-permute-start.23 = (bf16[4096,512]{1,0:T(8,128)(2,1)}, bf16[4096,512]{1,0:T(8,128)(2,1)}, u32[]{:S(2)}, u32[]{:S(2)}) collective-permute-start(bf16[4096,512]{1,0:T(8,128)(2,1)} %pad_maximum_fusion), channel_id=1, source_target_pairs={{0,1},{1,0},{2,3},{3,2},{4,5},{5,4},{6,7},{7,6},{8,9},{9,8},{10,11... | collective-permute-start | bytes 12582920 | tf_op jit(solution)/shard_map/ppermute | solution.py:342
  207.7 13.5 %collective-permute-start.27 = (bf16[512,512]{1,0:T(8,128)(2,1)S(1)}, bf16[512,512]{1,0:T(8,128)(2,1)S(1)}, u32[]{:S(2)}, u32[]{:S(2)}) collective-permute-start(bf16[512,512]{1,0:T(8,128)(2,1)S(1)} %pad_maximum_fusion.2), channel_id=1, source_target_pairs={{0,6},{1,7},{2,0},{3,1},{4,2},{5,3},{6,4},{7,5},{8,14},{9,15},{10,... | collective-permute-start | bytes 1572872 | tf_op jit(solution)/shard_map/ppermute | solution.py:365
  215.3 13.3 %collective-permute-start.25 = (bf16[512,512]{1,0:T(8,128)(2,1)S(1)}, bf16[512,512]{1,0:T(8,128)(2,1)S(1)}, u32[]{:S(2)}, u32[]{:S(2)}) collective-permute-start(bf16[512,512]{1,0:T(8,128)(2,1)S(1)} %pad_maximum_fusion.1), channel_id=1, source_target_pairs={{0,2},{1,3},{2,4},{3,5},{4,6},{5,7},{6,0},{7,1},{8,10},{9,11},{10,... | collective-permute-start | bytes 1572872 | tf_op jit(solution)/shard_map/ppermute | solution.py:364
  230.6 10.3 %all-to-all-start.2 = ((f32[8,1,512]{2,1,0:T(1,128)}), f32[8,1,512]{2,1,0:T(1,128)S(1)}, u32[]{:S(2)}, u32[]{:S(2)}) async-start(f32[8,1,512]{2,1,0:T(1,128)} %broadcast_in_dim.110), calls=%async_computation.2 | async-start | bytes 32768 | tf_op jit(solution)/shard_map/all_to_all | solution.py:29
  (20 other events, 347.5 us)

commit v4 on v3

--- a/solution.py
+++ b/solution.py
@@ -3,6 +3,7 @@
 
 import jax
 import jax.numpy as jnp
+import numpy as np
 from jax import lax
 from jax.experimental import pallas as pl
 from jax.experimental.pallas import tpu as pltpu
@@ -193,7 +194,7 @@
             ]
 
 
-def attend(table, visible, offsets, queries, drafts, sources, plan, window, per_step=2):
+def attend(table, visible, offsets, queries, drafts, sources, plan, window, per_step=4):
     requests, rows, head_dim = queries.shape
     slots = sum(length for _, _, length in plan)
     return pl.pallas_call(
@@ -234,6 +235,28 @@
     return starts, travelling
 
 
+def pack_table(capacity, y_len, ring_len, first_room):
+    fixed = {0: (0, 3, 6, 8), 1: (1, 4, 7, 9), ring_len - 1: (2, 5, 11, 10)}
+    kinds = y_len * ring_len
+    base = np.zeros((2 * kinds + 2,), np.int32)
+    weights = np.zeros((2 * kinds + 2, 3, kinds), np.int32)
+    for way, order in enumerate(((4, 3, 2), (4, 5, 6))):
+        earlier = []
+        for q in order:
+            for r in range(y_len):
+                d = r * ring_len + q
+                for parity in (way,) if q == 4 else (0, 1):
+                    base[2 * d + parity] = 12 * capacity + way * first_room
+                    for part, e in earlier:
+                        weights[2 * d + parity, part, e] = 1
+                earlier.append((1 + way if q == 4 else 0, d))
+    for q, places in fixed.items():
+        for r, place in enumerate(places):
+            d = r * ring_len + q
+            base[2 * d : 2 * d + 2] = place * capacity
+    return jnp.asarray(base), jnp.asarray(weights)
+
+
 def by_distance(near, up, down, axis):
     part = lambda array, g: lax.slice_in_dim(array, g, g + 1, axis=axis)
     tables = []
@@ -293,32 +316,37 @@
             return ((u, d)[direction], ("offset", number), length)
 
         found[0, t, 0], found[1, t, 0] = piece(0, 0), piece(1, 0)
-        forward = [piece(0, 1), piece(1, 1), piece(0, 2)]
-        backward = [piece(0, 3), piece(1, 3), piece(1, 2)]
+        forward = [piece(0, 1), piece(1, 1)]
+        backward = [piece(0, 3), piece(1, 3)]
+        plans = [forward, backward]
+        if t < 4:
+            forward.append(piece(0, 2))
+            backward.append(piece(1, 2))
+        else:
+            plans.append([piece(0, 2), piece(1, 2)])
+        passed_at = sum(n for _, _, n in forward)
         for plan, passing in ((forward, passing_forth), (backward, passing_back)):
             if passing is not None:
                 plan.append((passing[0], ("at", passing[1]), passing[2]))
-        needed = sorted({p[0] for p in forward + backward})
+        needed = sorted({p[0] for plan in plans for p in plan})
         renamed = [
-            [(needed.index(source), start, n) for source, start, n in plan]
-            for plan in (forward, backward)
+            [(needed.index(source), start, n) for source, start, n in plan] for plan in plans
         ]
-        send_forth, send_back = pick(offsets, [arrays[i] for i in needed], renamed)
+        send_forth, send_back, *across = pick(offsets, [arrays[i] for i in needed], renamed)
         f = keep(lax.ppermute(send_forth, "dp", forth))
         b = keep(lax.ppermute(send_back, "dp", back))
         found[0, t, 1], found[1, t, 1] = (f, ("at", 0), length), (f, ("at", length), length)
         found[0, t, 3], found[1, t, 3] = (b, ("at", 0), length), (b, ("at", length), length)
         if t > 2:
-            found[0, t - 1, 2] = (f, ("at", 3 * length), full)
-            found[1, t - 1, 2] = (b, ("at", 3 * length), full)
+            found[0, t - 1, 2] = (f, ("at", passed_at), full)
+            found[1, t - 1, 2] = (b, ("at", passed_at), full)
         passing_forth, passing_back = (f, 2 * length, length), (b, 2 * length, length)
     near_up, near_down = pick(offsets, arrays[:5], [for_up, for_down])
     near_up = keep(lax.ppermute(near_up, "dp", up))
     near_down = keep(lax.ppermute(near_down, "dp", down))
-    last_forth = lax.slice_in_dim(arrays[passing_forth[0]], 2 * half, 3 * half)
-    last_back = lax.slice_in_dim(arrays[passing_back[0]], 2 * half, 3 * half)
-    found[0, 4, 2] = (keep(lax.ppermute(last_forth, "dp", forth)), ("at", 0), half)
-    found[1, 4, 2] = (keep(lax.ppermute(last_back, "dp", back)), ("at", 0), half)
+    two_on = [(start, forth[middle][1]) for start, middle in forth]
+    last = keep(lax.ppermute(across[0], "dp", two_on))
+    found[0, 4, 2], found[1, 4, 2] = (last, ("at", 0), half), (last, ("at", half), half)
     plan = home + [(near_up, ("at", 0), 4 * full), (near_down, ("at", 0), 4 * full)]
     plan += [found[direction, t, r] for t in range(2, 5) for direction in range(2) for r in range(4)]
     return arrays, plan
@@ -398,19 +426,12 @@
     ahead = jnp.where(block_dest >= 0, ahead_y * ring_len + ahead_z, rank_count)
     steps = jnp.arange(rank_count, dtype=jnp.int32)
     counts = jnp.sum((ahead[None, :] == steps[:, None]).astype(jnp.int32), axis=1, dtype=jnp.int32)
-    starts, _ = ring_starts(counts.reshape(y_len, ring_len))
-    fixed = jnp.array([[0, 3, 6, 8], [1, 4, 7, 9], [2, 5, 11, 10]], jnp.int32) * capacity
-    near_slots = 12 * capacity
-    tables = by_distance(
-        [fixed[n : n + 1] for n in range(3)],
-        near_slots + starts[0],
-        near_slots + room[0] + starts[1],
-        0,
-    )
-    start = jnp.stack([table.T for table in tables], axis=-1).reshape(-1)
+    base, weights = pack_table(capacity, y_len, ring_len, room[0])
+    parts = jnp.stack([counts, over(counts + 1, 2), over(counts, 2)])
+    start = base + jnp.sum(weights * parts[None], axis=(1, 2), dtype=jnp.int32)
     outputs = pack_blocks(
         ahead,
-        jnp.concatenate([start, jnp.zeros((2,), jnp.int32)]),
+        start,
         pool,
         (3 * capacity, 5 * capacity, 4 * capacity, room[0], room[0]),
         lambda d: (d & (ring_len - 1)) == ring_len // 2,

time: 244 us -> 253 us (1.037)
  waiting for transfers between devices: 77.7 us -> 94.7 us
  local copies, waits for them, and re-layouts: 24.9 us -> 19.4 us
    ppermute x2, waiting for transfers between devices: 1.39 us -> 26.3 us  [along_rings(): falling = lax.ppermute(lax.slice_in_dim(falling, 0, room[t]), 'dp', down)]
    ppermute x3, waiting for transfers between devices: 31.6 us -> 14.7 us  [along_rings(): f = keep(lax.ppermute(send_forth, 'dp', forth))]
    ppermute x2 -> x1, waiting for transfers between devices: 1.94 us -> 11.1 us  [along_rings(): last = keep(lax.ppermute(across[0], 'dp', two_on))]
    ppermute x2 -> x1, starting transfers between devices: 2.82 us -> 0.28 us  [along_rings(): last = keep(lax.ppermute(across[0], 'dp', two_on))]
  transfers between devices with their start and end apart: 30 -> 29, of which waited for: 15 -> 12; matrix products, arithmetic and copies ran while one was open for 22% -> 20% of each run, Pallas kernels for 7% -> 7%
where the time goes in v4:
time: 253 us; the launch traced here: 252 us
  waiting for transfers between devices  94.7 us (37%)
  starting transfers between devices  59.3 us (23%)
  Pallas kernels  37.2 us (15%)
  other arithmetic  22.9 us (9%)
  local copies, waits for them, and re-layouts  19.4 us (8%)
  matrix products  16.7 us (7%)
    ppermute x2, waiting for transfers between devices, along_rings(): falling = lax.ppermute(lax.slice_in_dim(falling, 0, room[t]), 'dp', down)  26.3 us
    ppermute x2, waiting for transfers between devices, first_moves(): rising = lax.ppermute(rising, 'dp', up)  22.7 us
    all_to_all x2, starting transfers between devices, from_everyone(): lax.all_to_all(jnp.broadcast_to(array[None], (length, *array.shape)), axi...  17.6 us
    pallas_call x1, Pallas kernels, attend(): pl.pallas_call(functools.partial(attend_kernel, per_step, plan), out_shap...  17.1 us
    ppermute x3, waiting for transfers between devices, along_rings(): f = keep(lax.ppermute(send_forth, 'dp', forth))  14.7 us
    pallas_call x4, Pallas kernels, pick(): pl.pallas_call(functools.partial(pick_kernel, plans), out_shape=[jax.Shap...  11.8 us
    ppermute x1, waiting for transfers between devices, along_rings(): last = keep(lax.ppermute(across[0], 'dp', two_on))  11.1 us
    dot_general x4, matrix products, own_part(): own = jnp.dot(token_rows, own_weight[k], preferred_element_type=jnp.float32)  9 us
  transfers between devices with their start and end apart: 29, of which 12 were waited for; matrix products, arithmetic and copies ran while one was open for 20% of the time, Pallas kernels for 7%

profile of v4, /device:TPU:1, one launch (start us, length us, event | category | flops | bytes accessed | tf_op | source)
XLA Modules:
  0.0 251.5 jit_solution(15623159823480411445)
XLA Ops:
  1.5 12.0 %all-to-all-start.1 = ((s32[32,1,32]{2,1,0:T(1,128)}), s32[32,1,32]{2,1,0:T(1,128)S(1)}, u32[]{:S(2)}, u32[]{:S(2)}) async-start(s32[32,1,32]{2,1,0:T(1,128)} %broadcast_in_dim.103), calls=%async_computation.1 | async-start | bytes 32768 | tf_op jit(solution)/shard_map/all_to_all | solution.py:30
  15.6 8.3 %pack_blocks.3 = (bf16[96,32,128]{2,1,0:T(8,128)(2,1)S(1)}, bf16[160,32,128]{2,1,0:T(8,128)(2,1)}, bf16[128,32,128]{2,1,0:T(8,128)(2,1)}, bf16[168,32,128]{2,1,0:T(8,128)(2,1)}, bf16[168,32,128]{2,1,0:T(8,128)(2,1)}) custom-call(s32[512]{0:T(512)} %copy-done.4, s32[66]{0:T(128)} %add.194.start_ref, bf16[512,32,128]{2,1,0:T(8,128)(2,1)} %bitcast.42), custom_call_target="tpu_custom_call" | custom-call | flops 268435456 | bytes 8388608 | tf_op jit(solution)/shard_map/pack_blocks/pallas_call | solution.py:75
  34.1 2.5 constant_dynamic-slice_fusion.3
  41.0 15.3 %collective-permute-done.13 = bf16[168,32,128]{2,1,0:T(8,128)(2,1)} collective-permute-done((bf16[168,32,128]{2,1,0:T(8,128)(2,1)}, bf16[168,32,128]{2,1,0:T(8,128)(2,1)}, u32[]{:S(2)}, u32[]{:S(2)}) %collective-permute-start.13) | collective-permute-done | bytes 1376288 | tf_op jit(solution)/shard_map/ppermute | solution.py:283
  56.3 2.7 %collective-permute-start.16 = (bf16[168,32,128]{2,1,0:T(8,128)(2,1)}, bf16[168,32,128]{2,1,0:T(8,128)(2,1)S(1)}, u32[]{:S(2)}, u32[]{:S(2)}) collective-permute-start(bf16[168,32,128]{2,1,0:T(8,128)(2,1)} %collective-permute-done.15), channel_id=1, source_target_pairs={{0,56},{8,0},{16,8},{24,16},{32,24},{40,32},{48,40},{56,48},{64,12... | collective-permute-start | bytes 4128776 | tf_op jit(solution)/shard_map/ppermute | solution.py:284
  61.6 2.6 %select_reduce_fusion = (s32[32,32]{1,0:T(8,128)S(1)}, s32[32,32]{1,0:T(8,128)S(1)}, s32[32,32]{1,0:T(8,128)S(1)}) fusion(s32[32]{0:T(128)} %compare_convert_fusion.1, s32[32,32]{1,0:T(8,128)} %broadcast_shift-right-arithmetic_fusion, s32[32]{0:T(128)S(1)} %get-tuple-element.92, s32[32]{0:T(128)S(1)} %get-tuple-element.93), kind=kLoop, calls=%fused_computation.31 | loop fusion | flops 226304 | bytes 16768 | tf_op jit(solution)/shard_map/reduce_sum | solution.py:473
  80.3 7.4 %collective-permute-done.14 = bf16[168,32,128]{2,1,0:T(8,128)(2,1)S(1)} collective-permute-done((bf16[168,32,128]{2,1,0:T(8,128)(2,1)}, bf16[168,32,128]{2,1,0:T(8,128)(2,1)S(1)}, u32[]{:S(2)}, u32[]{:S(2)}) %collective-permute-start.14) | collective-permute-done | bytes 1376288 | tf_op jit(solution)/shard_map/ppermute | solution.py:283
  87.7 103.4 %conditional.1 = (bf16[512,1024]{1,0:T(8,128)(2,1)}) conditional(s32[]{:T(128)} %convert_element_type.59, (s32[32,32]{1,0:T(8,128)S(1)}, s32[512]{0:T(512)}, bf16[512,32,128]{2,1,0:T(8,128)(2,1)}, s32[32]{0:T(128)}, bf16[32,128,128]{2,1,0:T(8,128)(2,1)}, /*index=5*/bf16[32,32,128]{2,1,0:T(8,128)(2,1)}) %tuple.43, (s32[24]{0:T(128)}, ...), branch_computations={%region_14.15_spmd, %region_15.16_spmd} | conditional | flops 1342178304 | bytes 72893928 | solution.py:493
  90.2 2.3 collective-permute-start.3
  97.3 14.7 %collective-permute-done.refs_0_.refs_7_ = bf16[96,32,128]{2,1,0:T(8,128)(2,1)} collective-permute-done((bf16[96,32,128]{2,1,0:T(8,128)(2,1)}, bf16[96,32,128]{2,1,0:T(8,128)(2,1)}, u32[]{:S(2)}, u32[]{:S(2)}) %collective-permute-start) | collective-permute-done | bytes 786464 | tf_op jit(solution)/shard_map/cond/branch_1_fun/ppermute | solution.py:336
  112.5 3.5 %pick.5 = (bf16[128,32,128]{2,1,0:T(8,128)(2,1)}, bf16[128,32,128]{2,1,0:T(8,128)(2,1)}) custom-call(s32[24]{0:T(128)S(1)} %copy-done.5, bf16[96,32,128]{2,1,0:T(8,128)(2,1)} %collective-permute-done.refs_0_.refs_7_, bf16[96,32,128]{2,1,0:T(8,128)(2,1)} %collective-permute-done.1.refs_1_.refs_8_, ...), custom_call_target="tpu_custom_call" | custom-call | flops 1048576 | bytes 4194304 | tf_op jit(solution)/shard_map/cond/branch_1_fun/pick/pallas_call | solution.py:119
  122.7 3.3 %pick.7 = (bf16[128,32,128]{2,1,0:T(8,128)(2,1)}, bf16[128,32,128]{2,1,0:T(8,128)(2,1)}) custom-call(s32[24]{0:T(128)S(1)} %copy-done.5, bf16[96,32,128]{2,1,0:T(8,128)(2,1)S(1)} %get-tuple-element.55.refs_0_, bf16[160,32,128]{2,1,0:T(8,128)(2,1)} %get-tuple-element.56.refs_1_, bf16[128,32,128]{2,1,0:T(8,128)(2,1)} %get-tuple-element.57.refs_2_, ...), custom_call_target="tpu_custom_call" | custom-call | flops 1048576 | bytes 4194304 | tf_op jit(solution)/shard_map/cond/branch_1_fun/pick/pallas_call | solution.py:119
  130.7 25.8 %collective-permute-done.7.refs_3_.refs_14_ = bf16[52,32,128]{2,1,0:T(8,128)(2,1)} collective-permute-done((bf16[52,32,128]{2,1,0:T(8,128)(2,1)S(1)}, bf16[52,32,128]{2,1,0:T(8,128)(2,1)}, u32[]{:S(2)}, u32[]{:S(2)}) %collective-permute-start.7) | collective-permute-done | bytes 426016 | tf_op jit(solution)/shard_map/cond/branch_1_fun/ppermute | solution.py:311
  156.5 3.0 %pick.6 = (bf16[64,32,128]{2,1,0:T(8,128)(2,1)}, bf16[64,32,128]{2,1,0:T(8,128)(2,1)}, bf16[32,32,128]{2,1,0:T(8,128)(2,1)}) custom-call(s32[24]{0:T(128)S(1)} %copy-done.5, bf16[128,32,128]{2,1,0:T(8,128)(2,1)} %collective-permute-done.4.refs_0_.refs_11_, bf16[128,32,128]{2,1,0:T(8,128)(2,1)} %collective-permute-done.5.refs_1_.refs_12_, ...), custom_call_target="tpu_custom_call" | custom-call | flops 1048576 | bytes 4194304 | tf_op jit(solution)/shard_map/cond/branch_1_fun/pick/pallas_call | solution.py:119
  159.7 2.6 %collective-permute-start.9 = (bf16[64,32,128]{2,1,0:T(8,128)(2,1)}, bf16[64,32,128]{2,1,0:T(8,128)(2,1)}, u32[]{:S(2)}, u32[]{:S(2)}) collective-permute-start(bf16[64,32,128]{2,1,0:T(8,128)(2,1)} %get-tuple-element.67), channel_id=1, source_target_pairs={{0,192},{8,200},{16,208},{24,216},{32,224},{40,232},{48,240},{56,2... | collective-permute-start | bytes 1572872 | tf_op jit(solution)/shard_map/cond/branch_1_fun/ppermute | solution.py:337
  162.6 11.1 %collective-permute-done.12.refs_19_ = bf16[32,32,128]{2,1,0:T(8,128)(2,1)} collective-permute-done((bf16[32,32,128]{2,1,0:T(8,128)(2,1)}, bf16[32,32,128]{2,1,0:T(8,128)(2,1)}, u32[]{:S(2)}, u32[]{:S(2)}) %collective-permute-start.12) | collective-permute-done | bytes 262176 | tf_op jit(solution)/shard_map/cond/branch_1_fun/ppermute | solution.py:348
  173.7 17.1 %attend.3 = bf16[512,1024]{1,0:T(8,128)(2,1)} custom-call(s32[1024]{0:T(1024)S(1)} %copy-done.6, s32[32]{0:T(128)S(1)} %copy-done.10, s32[24]{0:T(128)S(1)} %copy-done.5, bf16[32,128,128]{2,1,0:T(8,128)(2,1)} %get-tuple-element.53.queries_ref, bf16[32,32,128]{2,1,0:T(8,128)(2,1)} %get-tuple-element.54.draft_ref, ...), custom_call_target="tpu_custom_call" | custom-call | flops 1073741824 | bytes 10485760 | tf_op jit(solution)/shard_map/cond/branch_1_fun/attend/pallas_call | solution.py:200
  191.1 7.5 %collective-permute-start.22 = (bf16[4096,512]{1,0:T(8,128)(2,1)}, bf16[4096,512]{1,0:T(8,128)(2,1)}, u32[]{:S(2)}, u32[]{:S(2)}) collective-permute-start(bf16[4096,512]{1,0:T(8,128)(2,1)} %pad_maximum_fusion), channel_id=1, source_target_pairs={{0,1},{1,0},{2,3},{3,2},{4,5},{5,4},{6,7},{7,6},{8,9},{9,8},{10,11... | collective-permute-start | bytes 12582920 | tf_op jit(solution)/shard_map/ppermute | solution.py:370
  209.3 2.6 %collective-permute-start.25 = (bf16[512,256]{1,0:T(8,128)(2,1)S(1)}, bf16[512,256]{1,0:T(8,128)(2,1)S(1)}, u32[]{:S(2)}, u32[]{:S(2)}) collective-permute-start(bf16[512,256]{1,0:T(8,128)(2,1)S(1)} %get-tuple-element.101), channel_id=1, source_target_pairs={{0,6},{1,7},{2,0},{3,1},{4,2},{5,3},{6,4},{7,5},{8,14},{9,15},{10,... | collective-permute-start | bytes 786440 | tf_op jit(solution)/shard_map/ppermute | solution.py:386
  217.3 3.5 %collective-permute-start.26 = (bf16[512,512]{1,0:T(8,128)(2,1)S(1)}, bf16[512,512]{1,0:T(8,128)(2,1)S(1)}, u32[]{:S(2)}, u32[]{:S(2)}) collective-permute-start(bf16[512,512]{1,0:T(8,128)(2,1)S(1)} %pad_maximum_fusion.2), channel_id=1, source_target_pairs={{0,6},{1,7},{2,0},{3,1},{4,2},{5,3},{6,4},{7,5},{8,14},{9,15},{10,... | collective-permute-start | bytes 1572872 | tf_op jit(solution)/shard_map/ppermute | solution.py:393
  220.8 4.0 %collective-permute-done.23 = bf16[512,256]{1,0:T(8,128)(2,1)S(1)} collective-permute-done((bf16[512,256]{1,0:T(8,128)(2,1)S(1)}, bf16[512,256]{1,0:T(8,128)(2,1)S(1)}, u32[]{:S(2)}, u32[]{:S(2)}) %collective-permute-start.23) | collective-permute-done | bytes 262176 | tf_op jit(solution)/shard_map/ppermute | solution.py:385
  230.8 7.3 %collective-permute-done.24 = bf16[512,512]{1,0:T(8,128)(2,1)S(1)} collective-permute-done((bf16[512,512]{1,0:T(8,128)(2,1)S(1)}, bf16[512,512]{1,0:T(8,128)(2,1)S(1)}, u32[]{:S(2)}, u32[]{:S(2)}) %collective-permute-start.24) | collective-permute-done | bytes 524320 | tf_op jit(solution)/shard_map/ppermute | solution.py:392
  240.2 5.6 %all-to-all-start.2 = ((f32[8,1,512]{2,1,0:T(1,128)}), f32[8,1,512]{2,1,0:T(1,128)S(1)}, u32[]{:S(2)}, u32[]{:S(2)}) async-start(f32[8,1,512]{2,1,0:T(1,128)} %broadcast_in_dim.111), calls=%async_computation.2 | async-start | bytes 32768 | tf_op jit(solution)/shard_map/all_to_all | solution.py:30
  246.0 4.5 %all-to-all-done.2 = f32[8,1,512]{2,1,0:T(1,128)S(1)} async-done(((f32[8,1,512]{2,1,0:T(1,128)}), f32[8,1,512]{2,1,0:T(1,128)S(1)}, u32[]{:S(2)}, u32[]{:S(2)}) %all-to-all-start.2) | async-done | bytes 16416 | tf_op jit(solution)/shard_map/all_to_all | solution.py:30
  (155 shorter events, 81.1 us)
Async XLA Ops:
  1.5 37.8 %all-to-all-start.1 = ((s32[32,1,32]{2,1,0:T(1,128)}), s32[32,1,32]{2,1,0:T(1,128)S(1)}, u32[]{:S(2)}, u32[]{:S(2)}) async-start(s32[32,1,32]{2,1,0:T(1,128)} %broadcast_in_dim.103), calls=%async_computation.1 | async-start | bytes 32768 | tf_op jit(solution)/shard_map/all_to_all | solution.py:30
  23.9 32.4 %collective-permute-start.13 = (bf16[168,32,128]{2,1,0:T(8,128)(2,1)}, bf16[168,32,128]{2,1,0:T(8,128)(2,1)}, u32[]{:S(2)}, u32[]{:S(2)}) collective-permute-start(bf16[168,32,128]{2,1,0:T(8,128)(2,1)} %get-tuple-element.83), channel_id=1, source_target_pairs={{0,8},{8,16},{16,24},{24,32},{32,40},{40,48},{48,56},{56,0},{64,72... | collective-permute-start | bytes 4128776 | tf_op jit(solution)/shard_map/ppermute | solution.py:283
  25.2 31.1 %collective-permute-start.15 = (bf16[168,32,128]{2,1,0:T(8,128)(2,1)}, bf16[168,32,128]{2,1,0:T(8,128)(2,1)}, u32[]{:S(2)}, u32[]{:S(2)}) collective-permute-start(bf16[168,32,128]{2,1,0:T(8,128)(2,1)} %get-tuple-element.84), channel_id=1, source_target_pairs={{0,56},{8,0},{16,8},{24,16},{32,24},{40,32},{48,40},{56,48},{64,12... | collective-permute-start | bytes 4128776 | tf_op jit(solution)/shard_map/ppermute | solution.py:284
  26.7 37.5 %collective-permute-start.17 = (bf16[160,32,128]{2,1,0:T(8,128)(2,1)}, bf16[160,32,128]{2,1,0:T(8,128)(2,1)}, u32[]{:S(2)}, u32[]{:S(2)}) collective-permute-start(bf16[160,32,128]{2,1,0:T(8,128)(2,1)} %get-tuple-element.86), channel_id=1, source_target_pairs={{0,64},{8,72},{16,80},{24,88},{32,96},{40,104},{48,112},{56,120},{... | collective-permute-start | bytes 3932168 | tf_op jit(solution)/shard_map/ppermute | solution.py:285
  27.9 39.7 %collective-permute-start.18 = (bf16[128,32,128]{2,1,0:T(8,128)(2,1)}, bf16[128,32,128]{2,1,0:T(8,128)(2,1)}, u32[]{:S(2)}, u32[]{:S(2)}) collective-permute-start(bf16[128,32,128]{2,1,0:T(8,128)(2,1)} %get-tuple-element.87), channel_id=1, source_target_pairs={{0,192},{8,200},{16,208},{24,216},{32,224},{40,232},{48,240},{56,2... | collective-permute-start | bytes 3145736 | tf_op jit(solution)/shard_map/ppermute | solution.py:286
  56.3 31.4 %collective-permute-start.14 = (bf16[168,32,128]{2,1,0:T(8,128)(2,1)}, bf16[168,32,128]{2,1,0:T(8,128)(2,1)S(1)}, u32[]{:S(2)}, u32[]{:S(2)}) collective-permute-start(bf16[168,32,128]{2,1,0:T(8,128)(2,1)} %collective-permute-done.13), channel_id=1, source_target_pairs={{0,8},{8,16},{16,24},{24,32},{32,40},{40,48},{48,56},{56,0},{64,72... | collective-permute-start | bytes 4128776 | tf_op jit(solution)/shard_map/ppermute | solution.py:283
  56.3 31.3 %collective-permute-start.16 = (bf16[168,32,128]{2,1,0:T(8,128)(2,1)}, bf16[168,32,128]{2,1,0:T(8,128)(2,1)S(1)}, u32[]{:S(2)}, u32[]{:S(2)}) collective-permute-start(bf16[168,32,128]{2,1,0:T(8,128)(2,1)} %collective-permute-done.15), channel_id=1, source_target_pairs={{0,56},{8,0},{16,8},{24,16},{32,24},{40,32},{48,40},{56,48},{64,12... | collective-permute-start | bytes 4128776 | tf_op jit(solution)/shard_map/ppermute | solution.py:284
  66.1 14.2 %collective-permute-start.19 = (bf16[64,32,128]{2,1,0:T(8,128)(2,1)}, bf16[64,32,128]{2,1,0:T(8,128)(2,1)}, u32[]{:S(2)}, u32[]{:S(2)}) collective-permute-start(bf16[64,32,128]{2,1,0:T(8,128)(2,1)} %slice.111), channel_id=1, source_target_pairs={{0,64},{8,72},{16,80},{24,88},{32,96},{40,104},{48,112},{56,120},{... | collective-permute-start | bytes 1572872 | tf_op jit(solution)/shard_map/ppermute | solution.py:287
  69.3 10.9 %collective-permute-start.20 = (bf16[32,32,128]{2,1,0:T(8,128)(2,1)}, bf16[32,32,128]{2,1,0:T(8,128)(2,1)}, u32[]{:S(2)}, u32[]{:S(2)}) collective-permute-start(bf16[32,32,128]{2,1,0:T(8,128)(2,1)} %slice.112), channel_id=1, source_target_pairs={{0,192},{8,200},{16,208},{24,216},{32,224},{40,232},{48,240},{56,2... | collective-permute-start | bytes 786440 | tf_op jit(solution)/shard_map/ppermute | solution.py:288
  88.7 23.3 %collective-permute-start.2 = (bf16[124,32,128]{2,1,0:T(8,128)(2,1)}, bf16[124,32,128]{2,1,0:T(8,128)(2,1)}, u32[]{:S(2)}, u32[]{:S(2)}) collective-permute-start(bf16[124,32,128]{2,1,0:T(8,128)(2,1)} %slice.21), channel_id=1, source_target_pairs={{0,8},{8,16},{16,24},{24,32},{32,40},{40,48},{48,56},{56,0},{64,72... | collective-permute-start | bytes 3047432 | tf_op jit(solution)/shard_map/cond/branch_1_fun/ppermute | solution.py:310
  90.2 22.3 %collective-permute-start.3 = (bf16[124,32,128]{2,1,0:T(8,128)(2,1)}, bf16[124,32,128]{2,1,0:T(8,128)(2,1)}, u32[]{:S(2)}, u32[]{:S(2)}) collective-permute-start(bf16[124,32,128]{2,1,0:T(8,128)(2,1)} %slice.22), channel_id=1, source_target_pairs={{0,56},{8,0},{16,8},{24,16},{32,24},{40,32},{48,40},{56,48},{64,12... | collective-permute-start | bytes 3047432 | tf_op jit(solution)/shard_map/cond/branch_1_fun/ppermute | solution.py:311
  94.5 17.5 %collective-permute-start = (bf16[96,32,128]{2,1,0:T(8,128)(2,1)}, bf16[96,32,128]{2,1,0:T(8,128)(2,1)}, u32[]{:S(2)}, u32[]{:S(2)}) collective-permute-start(bf16[96,32,128]{2,1,0:T(8,128)(2,1)} %get-tuple-element.62), channel_id=1, source_target_pairs={{0,64},{8,72},{16,80},{24,88},{32,96},{40,104},{48,112},{56,120},{... | collective-permute-start | bytes 2359304 | tf_op jit(solution)/shard_map/cond/branch_1_fun/ppermute | solution.py:336
  95.2 16.7 %collective-permute-start.1 = (bf16[96,32,128]{2,1,0:T(8,128)(2,1)}, bf16[96,32,128]{2,1,0:T(8,128)(2,1)}, u32[]{:S(2)}, u32[]{:S(2)}) collective-permute-start(bf16[96,32,128]{2,1,0:T(8,128)(2,1)} %get-tuple-element.63), channel_id=1, source_target_pairs={{0,192},{8,200},{16,208},{24,216},{32,224},{40,232},{48,240},{56,2... | collective-permute-start | bytes 2359304 | tf_op jit(solution)/shard_map/cond/branch_1_fun/ppermute | solution.py:337
  116.0 40.6 %collective-permute-start.4 = (bf16[128,32,128]{2,1,0:T(8,128)(2,1)}, bf16[128,32,128]{2,1,0:T(8,128)(2,1)}, u32[]{:S(2)}, u32[]{:S(2)}) collective-permute-start(bf16[128,32,128]{2,1,0:T(8,128)(2,1)} %get-tuple-element.64), channel_id=1, source_target_pairs={{0,64},{8,72},{16,80},{24,88},{32,96},{40,104},{48,112},{56,120},{... | collective-permute-start | bytes 3145736 | tf_op jit(solution)/shard_map/cond/branch_1_fun/ppermute | solution.py:336
  117.2 39.3 %collective-permute-start.5 = (bf16[128,32,128]{2,1,0:T(8,128)(2,1)}, bf16[128,32,128]{2,1,0:T(8,128)(2,1)}, u32[]{:S(2)}, u32[]{:S(2)}) collective-permute-start(bf16[128,32,128]{2,1,0:T(8,128)(2,1)} %get-tuple-element.65), channel_id=1, source_target_pairs={{0,192},{8,200},{16,208},{24,216},{32,224},{40,232},{48,240},{56,2... | collective-permute-start | bytes 3145736 | tf_op jit(solution)/shard_map/cond/branch_1_fun/ppermute | solution.py:337
  126.0 36.6 %collective-permute-start.10 = (bf16[128,32,128]{2,1,0:T(8,128)(2,1)}, bf16[128,32,128]{2,1,0:T(8,128)(2,1)}, u32[]{:S(2)}, u32[]{:S(2)}) collective-permute-start(bf16[128,32,128]{2,1,0:T(8,128)(2,1)} %get-tuple-element.68), channel_id=1, source_target_pairs={{0,8},{8,16},{16,24},{24,32},{32,40},{40,48},{48,56},{56,0},{64,72... | collective-permute-start | bytes 3145736 | tf_op jit(solution)/shard_map/cond/branch_1_fun/ppermute | solution.py:345
  127.2 35.3 %collective-permute-start.11 = (bf16[128,32,128]{2,1,0:T(8,128)(2,1)}, bf16[128,32,128]{2,1,0:T(8,128)(2,1)}, u32[]{:S(2)}, u32[]{:S(2)}) collective-permute-start(bf16[128,32,128]{2,1,0:T(8,128)(2,1)} %get-tuple-element.69), channel_id=1, source_target_pairs={{0,56},{8,0},{16,8},{24,16},{32,24},{40,32},{48,40},{56,48},{64,12... | collective-permute-start | bytes 3145736 | tf_op jit(solution)/shard_map/cond/branch_1_fun/ppermute | solution.py:346
  129.8 26.7 %collective-permute-start.7 = (bf16[52,32,128]{2,1,0:T(8,128)(2,1)S(1)}, bf16[52,32,128]{2,1,0:T(8,128)(2,1)}, u32[]{:S(2)}, u32[]{:S(2)}) collective-permute-start(bf16[52,32,128]{2,1,0:T(8,128)(2,1)S(1)} %slice.99), channel_id=1, source_target_pairs={{0,56},{8,0},{16,8},{24,16},{32,24},{40,32},{48,40},{56,48},{64,12... | collective-permute-start | bytes 1277960 | tf_op jit(solution)/shard_map/cond/branch_1_fun/ppermute | solution.py:311
  159.5 14.1 %collective-permute-start.8 = (bf16[64,32,128]{2,1,0:T(8,128)(2,1)}, bf16[64,32,128]{2,1,0:T(8,128)(2,1)}, u32[]{:S(2)}, u32[]{:S(2)}) collective-permute-start(bf16[64,32,128]{2,1,0:T(8,128)(2,1)} %get-tuple-element.66), channel_id=1, source_target_pairs={{0,64},{8,72},{16,80},{24,88},{32,96},{40,104},{48,112},{56,120},{... | collective-permute-start | bytes 1572872 | tf_op jit(solution)/shard_map/cond/branch_1_fun/ppermute | solution.py:336
  159.7 13.9 %collective-permute-start.9 = (bf16[64,32,128]{2,1,0:T(8,128)(2,1)}, bf16[64,32,128]{2,1,0:T(8,128)(2,1)}, u32[]{:S(2)}, u32[]{:S(2)}) collective-permute-start(bf16[64,32,128]{2,1,0:T(8,128)(2,1)} %get-tuple-element.67), channel_id=1, source_target_pairs={{0,192},{8,200},{16,208},{24,216},{32,224},{40,232},{48,240},{56,2... | collective-permute-start | bytes 1572872 | tf_op jit(solution)/shard_map/cond/branch_1_fun/ppermute | solution.py:337
  162.3 11.4 %collective-permute-start.12 = (bf16[32,32,128]{2,1,0:T(8,128)(2,1)}, bf16[32,32,128]{2,1,0:T(8,128)(2,1)}, u32[]{:S(2)}, u32[]{:S(2)}) collective-permute-start(bf16[32,32,128]{2,1,0:T(8,128)(2,1)} %get-tuple-element.70), channel_id=1, source_target_pairs={{0,128},{8,136},{16,144},{24,152},{32,160},{40,168},{48,176},{56,1... | collective-permute-start | bytes 786440 | tf_op jit(solution)/shard_map/cond/branch_1_fun/ppermute | solution.py:348
  191.1 16.0 %collective-permute-start.22 = (bf16[4096,512]{1,0:T(8,128)(2,1)}, bf16[4096,512]{1,0:T(8,128)(2,1)}, u32[]{:S(2)}, u32[]{:S(2)}) collective-permute-start(bf16[4096,512]{1,0:T(8,128)(2,1)} %pad_maximum_fusion), channel_id=1, source_target_pairs={{0,1},{1,0},{2,3},{3,2},{4,5},{5,4},{6,7},{7,6},{8,9},{9,8},{10,11... | collective-permute-start | bytes 12582920 | tf_op jit(solution)/shard_map/ppermute | solution.py:370
  217.3 13.5 %collective-permute-start.26 = (bf16[512,512]{1,0:T(8,128)(2,1)S(1)}, bf16[512,512]{1,0:T(8,128)(2,1)S(1)}, u32[]{:S(2)}, u32[]{:S(2)}) collective-permute-start(bf16[512,512]{1,0:T(8,128)(2,1)S(1)} %pad_maximum_fusion.2), channel_id=1, source_target_pairs={{0,6},{1,7},{2,0},{3,1},{4,2},{5,3},{6,4},{7,5},{8,14},{9,15},{10,... | collective-permute-start | bytes 1572872 | tf_op jit(solution)/shard_map/ppermute | solution.py:393
  224.9 13.3 %collective-permute-start.24 = (bf16[512,512]{1,0:T(8,128)(2,1)S(1)}, bf16[512,512]{1,0:T(8,128)(2,1)S(1)}, u32[]{:S(2)}, u32[]{:S(2)}) collective-permute-start(bf16[512,512]{1,0:T(8,128)(2,1)S(1)} %pad_maximum_fusion.1), channel_id=1, source_target_pairs={{0,2},{1,3},{2,4},{3,5},{4,6},{5,7},{6,0},{7,1},{8,10},{9,11},{10,... | collective-permute-start | bytes 1572872 | tf_op jit(solution)/shard_map/ppermute | solution.py:392
  (17 other events, 372.5 us)
